TPU v7x, 256 devices: a whole 4x4x8 slice. The times are simulated.
256 devices in a mesh: gx: 4 (over x), gy: 4 (over y), gz: 16 (over z, core).
Axes of the slice: x: 4, y: 4, z: 8, core: 2. Of those that a mesh axis runs over, the one named last changes fastest.
Arguments:
- embeds: bfloat16 [2048, 128, 2048], P(('gx', 'gy', 'gz')), may hold values from -6 to 6
- dest_device: int32 [2048], P(('gx', 'gy', 'gz')), may hold values from 0 to 255, as said below
- shuffle_key: int32 [2048], P(('gx', 'gy', 'gz')), may hold values from 0 to 2047, each once
- lengths: int32 [64], replicated, may hold values from 1 to 4096
- gain: float32 [2048], replicated, may hold values from 0.1 to 1.9
Outputs:
- packed: bfloat16 [4096, 128, 2048], P(('gx', 'gy', 'gz'))
Inputs may be any that keep to these rules, and one draw needn't show every extreme that they name: `dest_device`: device numbers are ((gx * 4) + gy) * 16 + gz. A device receives at most 16 tiles, and in every draw some devices receive exactly 16. The 16 devices sharing gx and gy send at most one tile to any one device and exactly 8 tiles to the devices of each gz index. Of one device's tiles at most 1 go to devices of one gz index, and some device reaches that.
All inputs are finite; a program needn't handle non-finite values.
Results may differ from a plain program's by a relative error of at most 0.001.
Values may be sent and summed in bfloat16 or wider, within the bound.
No kernel may reach another device: no remote copies, remote signals or barrier semaphores. Data moves between devices by JAX's collectives and lax.ppermute only.
A program may use at most 128 MiB of HBM per device.

v0:
```python
import jax
import jax.numpy as jnp
from jax import lax
from jax.sharding import PartitionSpec as P

TILES_SEQ = 32


def in_blocks(array, dim, devices):
    before, after = (array.shape[:dim], array.shape[dim + 1 :])
    return jnp.moveaxis(array.reshape(*before, devices, -1, *after), dim, 0)


def edges_of(length, count):
    unit = 8 if length >= 8 * count else 1
    return [length // unit * k // count * unit for k in range(1, count)]


def joined_along(tiles, dim):
    tiles = jnp.moveaxis(tiles, 0, dim)
    shape = tiles.shape
    return tiles.reshape(*shape[:dim], shape[dim] * shape[dim + 1], *shape[dim + 2 :])


def cut_exchange(array, axis, pieces, split_dim, concat_dim):
    tiles = in_blocks(array, split_dim, lax.axis_size(axis))
    cut = max(range(1, max(2, tiles.ndim - 1)), key=lambda d: tiles.shape[d])
    gathered = []
    for piece in jnp.split(tiles, edges_of(tiles.shape[cut], pieces), axis=cut):
        if piece.size:
            gathered.append(lax.all_to_all(piece, axis, split_axis=0, concat_axis=0, tiled=True))
    return joined_along(jnp.concatenate(gathered, axis=cut), concat_dim)


def normalize(rows, tile_ids, lengths, gain):
    rows_tile = rows.shape[1]
    values = rows.astype(jnp.float32)
    meansq = jnp.mean(values * values, axis=-1, keepdims=True)
    scaled = values * lax.rsqrt(jnp.maximum(meansq, 0.25)) * gain
    seq_ids = tile_ids // TILES_SEQ
    match = seq_ids[:, None] == jnp.arange(lengths.shape[0], dtype=jnp.int32)[None, :]
    limit = jnp.sum(jnp.where(match, lengths[None, :], 0), axis=1)
    position = (tile_ids % TILES_SEQ)[:, None] * rows_tile + jnp.arange(rows_tile, dtype=jnp.int32)[
        None, :
    ]
    keep = position < limit[:, None]
    return jnp.where(keep[:, :, None], scaled, 0.0).astype(jnp.bfloat16)


def place(table, rows, numbers):
    moved = jnp.einsum(
        "sk,krd->srd", table.astype(jnp.bfloat16), rows, preferred_element_type=jnp.float32
    ).astype(jnp.bfloat16)
    picked = tuple(
        (
            jnp.sum(jnp.where(table, values[None, :] + 1, 0), axis=1).astype(jnp.int32) - 1
            for values in numbers
        )
    )
    return (moved, picked)


def shards(embeds, dest_device, shuffle_key, lengths, gain):
    tiles_here = embeds.shape[0]
    depth_count = lax.axis_size("gz")
    group_count = lax.axis_size("gx") * lax.axis_size("gy")
    device_index = (
        lax.axis_index("gx") * lax.axis_size("gy") + lax.axis_index("gy")
    ) * depth_count + lax.axis_index("gz")
    tile_ids = device_index * tiles_here + jnp.arange(tiles_here, dtype=jnp.int32)
    payload = normalize(embeds, tile_ids, lengths, gain)
    per_peer = (tiles_here + depth_count - 1) // depth_count
    first_slots = (
        dest_device % depth_count * per_peer
        + jnp.arange(tiles_here, dtype=jnp.int32) // depth_count
    )
    first_table = (
        jnp.arange(depth_count * per_peer, dtype=jnp.int32)[:, None] == first_slots[None, :]
    )
    first_rows, first_numbers = place(first_table, payload, (dest_device, shuffle_key, tile_ids))
    arrived_rows, arrived_dests, arrived_keys, arrived_ids = (
        cut_exchange(first_rows, "gz", 2, 0, 0),
        cut_exchange(first_numbers[0], "gz", 2, 0, 0),
        cut_exchange(first_numbers[1], "gz", 2, 0, 0),
        cut_exchange(first_numbers[2], "gz", 2, 0, 0),
    )
    second_slots = jnp.where(arrived_dests >= 0, arrived_dests // depth_count, -1)
    second_table = jnp.arange(group_count, dtype=jnp.int32)[:, None] == second_slots[None, :]
    second_rows, second_numbers = place(
        second_table, arrived_rows, (arrived_dests, arrived_keys, arrived_ids)
    )
    final_rows, final_dests, final_keys, final_ids = (
        cut_exchange(second_rows, ("gx", "gy"), 2, 0, 0),
        cut_exchange(second_numbers[0], ("gx", "gy"), 2, 0, 0),
        cut_exchange(second_numbers[1], ("gx", "gy"), 2, 0, 0),
        cut_exchange(second_numbers[2], ("gx", "gy"), 2, 0, 0),
    )
    valid = final_dests >= 0
    earlier = valid[None, :] & valid[:, None] & (final_keys[None, :] < final_keys[:, None])
    rank = jnp.sum(earlier.astype(jnp.int32), axis=1)
    final_slots = jnp.where(valid, rank, -1)
    final_table = jnp.arange(2 * tiles_here, dtype=jnp.int32)[:, None] == final_slots[None, :]
    packed_rows, packed_numbers = place(final_table, final_rows, (final_ids,))
    return packed_rows


def solution(mesh):
    return jax.shard_map(
        shards,
        mesh=mesh,
        in_specs=(
            P(("gx", "gy", "gz"), None, None),
            P(("gx", "gy", "gz")),
            P(("gx", "gy", "gz")),
            P(),
            P(),
        ),
        out_specs=P(("gx", "gy", "gz"), None, None),
        check_vma=False,
    )
```

profile of v0, /device:TPU:32, one launch (start us, length us, event | category | flops | bytes accessed | tf_op | source)
XLA Modules:
  0.0 415.9 jit_solution(13242028396514674238)
XLA Ops:
  0.0 0.7 broadcast_add_fusion.2
  0.7 0.1 select_reduce_fusion.3
  0.8 0.7 copy.38
  1.5 8.6 %all-to-all-start.2 = ((s32[16,1,1]{2,1,0:T(1,128)}), s32[16,1,1]{2,1,0:T(1,128)S(1)}, u32[]{:S(2)}, u32[]{:S(2)}) async-start(s32[16,1,1]{2,1,0:T(1,128)} %copy.38), calls=%async_computation.2 | async-start | bytes 16384 | tf_op jit(solution)/shard_map/all_to_all | solution.py:31
  10.1 3.2 fusion
  13.3 0.0 copy-done.4
  13.3 0.2 select_reduce_fusion.2
  13.5 0.1 add_compare_fusion
  13.6 0.0 copy-done.3
  13.6 1.4 fusion.3
  15.0 5.6 %convert_bitcast_fusion.1 = bf16[16,1,128,2048]{3,0,2,1:T(8,128)(2,1)S(1)} fusion(bf16[8,128,2048]{2,1,0:T(8,128)(2,1)S(1)} %fusion.3, s32[8]{0:T(128)S(1)} %get-tuple-element.16), kind=kOutput, calls=%fused_computation.15 | convolution fusion | flops 71303296 | bytes 12582944 | tf_op jit(solution)/shard_map/sk,krd->srd/dot_general | solution.py:51
  20.6 3.7 fusion.27
  24.3 0.7 copy.36
  25.0 0.0 all-to-all-done.2
  25.0 7.2 %all-to-all-start = ((s32[16,1,1]{2,1,0:T(1,128)}), s32[16,1,1]{2,1,0:T(1,128)S(1)}, u32[]{:S(2)}, u32[]{:S(2)}) async-start(s32[16,1,1]{2,1,0:T(1,128)} %copy.36), calls=%async_computation | async-start | bytes 16384 | tf_op jit(solution)/shard_map/all_to_all | solution.py:31
  32.2 6.5 %copy.41 = bf16[16,1,64,2048]{3,2,1,0:T(8,128)(2,1)} copy(bf16[16,1,64,2048]{3,0,2,1:T(8,128)(2,1)} %get-tuple-element.11) | data formatting | bytes 8388608 | tf_op jit(solution)/shard_map/split | solution.py:29
  38.7 0.0 all-to-all-done
  38.7 7.2 %all-to-all-start.4 = ((bf16[16,1,64,2048]{3,2,1,0:T(8,128)(2,1)}), bf16[16,1,64,2048]{3,2,1,0:T(8,128)(2,1)}, u32[]{:S(2)}, u32[]{:S(2)}) async-start(bf16[16,1,64,2048]{3,2,1,0:T(8,128)(2,1)} %copy.41), calls=%async_computation.4 | async-start | bytes 8388608 | tf_op jit(solution)/shard_map/all_to_all | solution.py:31
  45.9 6.5 %copy.42 = bf16[16,1,64,2048]{3,2,1,0:T(8,128)(2,1)} copy(bf16[16,1,64,2048]{3,0,2,1:T(8,128)(2,1)} %get-tuple-element.12) | data formatting | bytes 8388608 | tf_op jit(solution)/shard_map/split | solution.py:29
  52.4 85.8 %all-to-all-done.4 = bf16[16,1,64,2048]{3,2,1,0:T(8,128)(2,1)} async-done(((bf16[16,1,64,2048]{3,2,1,0:T(8,128)(2,1)}), bf16[16,1,64,2048]{3,2,1,0:T(8,128)(2,1)}, u32[]{:S(2)}, u32[]{:S(2)}) %all-to-all-start.4) | async-done | bytes 4194336 | tf_op jit(solution)/shard_map/all_to_all | solution.py:31
  138.2 6.7 %all-to-all-start.5 = ((bf16[16,1,64,2048]{3,2,1,0:T(8,128)(2,1)}), bf16[16,1,64,2048]{3,2,1,0:T(8,128)(2,1)}, u32[]{:S(2)}, u32[]{:S(2)}) async-start(bf16[16,1,64,2048]{3,2,1,0:T(8,128)(2,1)} %copy.42), calls=%async_computation.5 | async-start | bytes 8388608 | tf_op jit(solution)/shard_map/all_to_all | solution.py:31
  144.9 0.4 reduce
  145.3 0.4 add_reduce_fusion
  145.7 0.1 select_reduce_fusion
  145.8 0.7 copy.37
  146.5 0.7 copy.39
  147.2 6.5 %copy.43 = bf16[16,1,64,2048]{3,0,2,1:T(8,128)(2,1)} copy(bf16[16,1,64,2048]{3,2,1,0:T(8,128)(2,1)} %all-to-all-done.4) | data formatting | bytes 8388608 | tf_op jit(solution)/shard_map/all_to_all | solution.py:31
  153.6 83.5 %all-to-all-done.5 = bf16[16,1,64,2048]{3,2,1,0:T(8,128)(2,1)} async-done(((bf16[16,1,64,2048]{3,2,1,0:T(8,128)(2,1)}), bf16[16,1,64,2048]{3,2,1,0:T(8,128)(2,1)}, u32[]{:S(2)}, u32[]{:S(2)}) %all-to-all-start.5) | async-done | bytes 4194336 | tf_op jit(solution)/shard_map/all_to_all | solution.py:31
  237.2 7.0 %all-to-all-start.3 = ((s32[16,1,1]{2,1,0:T(1,128)}), s32[16,1,1]{2,1,0:T(1,128)S(1)}, u32[]{:S(2)}, u32[]{:S(2)}) async-start(s32[16,1,1]{2,1,0:T(1,128)} %copy.39), calls=%async_computation.3 | async-start | bytes 16384 | tf_op jit(solution)/shard_map/all_to_all | solution.py:31
  244.2 4.6 %copy.44 = bf16[16,1,64,2048]{3,0,2,1:T(8,128)(2,1)S(1)} copy(bf16[16,1,64,2048]{3,2,1,0:T(8,128)(2,1)} %all-to-all-done.5) | data formatting | bytes 8388608 | tf_op jit(solution)/shard_map/all_to_all | solution.py:31
  248.9 2.5 convert_bitcast_fusion
  251.4 3.7 fusion.26
  255.1 0.0 all-to-all-done.3
  255.1 7.2 %all-to-all-start.1 = ((s32[16,1,1]{2,1,0:T(1,128)}), s32[16,1,1]{2,1,0:T(1,128)S(1)}, u32[]{:S(2)}, u32[]{:S(2)}) async-start(s32[16,1,1]{2,1,0:T(1,128)} %copy.37), calls=%async_computation.1 | async-start | bytes 16384 | tf_op jit(solution)/shard_map/all_to_all | solution.py:31
  262.3 6.5 %copy.45 = bf16[16,1,64,2048]{3,2,1,0:T(8,128)(2,1)} copy(bf16[16,1,64,2048]{3,0,2,1:T(8,128)(2,1)} %get-tuple-element.9) | data formatting | bytes 8388608 | tf_op jit(solution)/shard_map/split | solution.py:29
  268.8 1.1 all-to-all-done.1
  269.9 6.1 %all-to-all-start.6 = ((bf16[16,1,64,2048]{3,2,1,0:T(8,128)(2,1)}), bf16[16,1,64,2048]{3,2,1,0:T(8,128)(2,1)}, u32[]{:S(2)}, u32[]{:S(2)}) async-start(bf16[16,1,64,2048]{3,2,1,0:T(8,128)(2,1)} %copy.45), calls=%async_computation.6 | async-start | bytes 8388608 | tf_op jit(solution)/shard_map/all_to_all | solution.py:31
  276.1 6.5 %copy.46 = bf16[16,1,64,2048]{3,2,1,0:T(8,128)(2,1)} copy(bf16[16,1,64,2048]{3,0,2,1:T(8,128)(2,1)} %get-tuple-element.10) | data formatting | bytes 8388608 | tf_op jit(solution)/shard_map/split | solution.py:29
  282.6 47.9 %all-to-all-done.6 = bf16[16,1,64,2048]{3,2,1,0:T(8,128)(2,1)} async-done(((bf16[16,1,64,2048]{3,2,1,0:T(8,128)(2,1)}), bf16[16,1,64,2048]{3,2,1,0:T(8,128)(2,1)}, u32[]{:S(2)}, u32[]{:S(2)}) %all-to-all-start.6) | async-done | bytes 4194336 | tf_op jit(solution)/shard_map/all_to_all | solution.py:31
  330.5 11.4 %all-to-all-start.7 = ((bf16[16,1,64,2048]{3,2,1,0:T(8,128)(2,1)}), bf16[16,1,64,2048]{3,2,1,0:T(8,128)(2,1)}, u32[]{:S(2)}, u32[]{:S(2)}) async-start(bf16[16,1,64,2048]{3,2,1,0:T(8,128)(2,1)} %copy.46), calls=%async_computation.7 | async-start | bytes 8388608 | tf_op jit(solution)/shard_map/all_to_all | solution.py:31
  341.9 0.4 reduce.3
  342.3 0.4 compare_reduce_fusion
  342.6 0.2 convert_reduce_fusion
  342.8 6.5 %copy.47 = bf16[16,1,64,2048]{3,0,2,1:T(8,128)(2,1)} copy(bf16[16,1,64,2048]{3,2,1,0:T(8,128)(2,1)} %all-to-all-done.6) | data formatting | bytes 8388608 | tf_op jit(solution)/shard_map/all_to_all | solution.py:31
  349.3 45.9 %all-to-all-done.7 = bf16[16,1,64,2048]{3,2,1,0:T(8,128)(2,1)} async-done(((bf16[16,1,64,2048]{3,2,1,0:T(8,128)(2,1)}), bf16[16,1,64,2048]{3,2,1,0:T(8,128)(2,1)}, u32[]{:S(2)}, u32[]{:S(2)}) %all-to-all-start.7) | async-done | bytes 4194336 | tf_op jit(solution)/shard_map/all_to_all | solution.py:31
  395.2 4.6 %copy.48 = bf16[16,1,64,2048]{3,0,2,1:T(8,128)(2,1)S(1)} copy(bf16[16,1,64,2048]{3,2,1,0:T(8,128)(2,1)} %all-to-all-done.7) | data formatting | bytes 8388608 | tf_op jit(solution)/shard_map/all_to_all | solution.py:31
  399.9 4.6 %fusion.10 = bf16[16,128,2048]{2,0,1:T(8,128)(2,1)} fusion(bf16[16,1,64,2048]{3,0,2,1:T(8,128)(2,1)S(1)} %copy.48, bf16[16,1,64,2048]{3,0,2,1:T(8,128)(2,1)S(1)} %copy-done.2, s32[16]{0:T(128)S(1)} %broadcast_select_fusion), kind=kOutput, calls=%fused_computation.16 | convolution fusion | flops 155189504 | bytes 16777280 | tf_op jit(solution)/shard_map/sk,krd->srd/dot_general | solution.py:51
  404.5 11.4 %copy.49 = bf16[16,128,2048]{2,1,0:T(8,128)(2,1)} copy(bf16[16,128,2048]{2,0,1:T(8,128)(2,1)} %fusion.10) | data formatting | bytes 16777216 | tf_op jit(solution)/shard_map/convert_element_type | solution.py:53
  (16 shorter events, 0.1 us)
Async XLA Ops:
  0.0 13.3 %copy-start.4 = (s32[64]{0:T(128)S(1)}, s32[64]{0:T(128)}, u32[]{:S(2)}) copy-start(s32[64]{0:T(128)} %param.8) | copy-start | bytes 772
  0.0 13.6 %copy-start.3 = (f32[2048]{0:T(1024)S(1)}, f32[2048]{0:T(1024)}, u32[]{:S(2)}) copy-start(f32[2048]{0:T(1024)} %param.9) | copy-start | bytes 24580
  1.5 23.5 %all-to-all-start.2 = ((s32[16,1,1]{2,1,0:T(1,128)}), s32[16,1,1]{2,1,0:T(1,128)S(1)}, u32[]{:S(2)}, u32[]{:S(2)}) async-start(s32[16,1,1]{2,1,0:T(1,128)} %copy.38), calls=%async_computation.2 | async-start | bytes 16384 | tf_op jit(solution)/shard_map/all_to_all | solution.py:31
  10.1 3.5 copy-start
  25.0 13.7 %all-to-all-start = ((s32[16,1,1]{2,1,0:T(1,128)}), s32[16,1,1]{2,1,0:T(1,128)S(1)}, u32[]{:S(2)}, u32[]{:S(2)}) async-start(s32[16,1,1]{2,1,0:T(1,128)} %copy.36), calls=%async_computation | async-start | bytes 16384 | tf_op jit(solution)/shard_map/all_to_all | solution.py:31
  38.7 99.5 %all-to-all-start.4 = ((bf16[16,1,64,2048]{3,2,1,0:T(8,128)(2,1)}), bf16[16,1,64,2048]{3,2,1,0:T(8,128)(2,1)}, u32[]{:S(2)}, u32[]{:S(2)}) async-start(bf16[16,1,64,2048]{3,2,1,0:T(8,128)(2,1)} %copy.41), calls=%async_computation.4 | async-start | bytes 8388608 | tf_op jit(solution)/shard_map/all_to_all | solution.py:31
  138.2 99.0 %all-to-all-start.5 = ((bf16[16,1,64,2048]{3,2,1,0:T(8,128)(2,1)}), bf16[16,1,64,2048]{3,2,1,0:T(8,128)(2,1)}, u32[]{:S(2)}, u32[]{:S(2)}) async-start(bf16[16,1,64,2048]{3,2,1,0:T(8,128)(2,1)} %copy.42), calls=%async_computation.5 | async-start | bytes 8388608 | tf_op jit(solution)/shard_map/all_to_all | solution.py:31
  237.2 17.9 %all-to-all-start.3 = ((s32[16,1,1]{2,1,0:T(1,128)}), s32[16,1,1]{2,1,0:T(1,128)S(1)}, u32[]{:S(2)}, u32[]{:S(2)}) async-start(s32[16,1,1]{2,1,0:T(1,128)} %copy.39), calls=%async_computation.3 | async-start | bytes 16384 | tf_op jit(solution)/shard_map/all_to_all | solution.py:31
  244.2 4.6 %copy-start.1 = (bf16[16,1,64,2048]{3,0,2,1:T(8,128)(2,1)S(1)}, bf16[16,1,64,2048]{3,0,2,1:T(8,128)(2,1)}, u32[]{:S(2)}) copy-start(bf16[16,1,64,2048]{3,0,2,1:T(8,128)(2,1)} %copy.43) | copy-start | bytes 12582916
  255.1 14.8 %all-to-all-start.1 = ((s32[16,1,1]{2,1,0:T(1,128)}), s32[16,1,1]{2,1,0:T(1,128)S(1)}, u32[]{:S(2)}, u32[]{:S(2)}) async-start(s32[16,1,1]{2,1,0:T(1,128)} %copy.37), calls=%async_computation.1 | async-start | bytes 16384 | tf_op jit(solution)/shard_map/all_to_all | solution.py:31
  269.9 60.6 %all-to-all-start.6 = ((bf16[16,1,64,2048]{3,2,1,0:T(8,128)(2,1)}), bf16[16,1,64,2048]{3,2,1,0:T(8,128)(2,1)}, u32[]{:S(2)}, u32[]{:S(2)}) async-start(bf16[16,1,64,2048]{3,2,1,0:T(8,128)(2,1)} %copy.45), calls=%async_computation.6 | async-start | bytes 8388608 | tf_op jit(solution)/shard_map/all_to_all | solution.py:31
  330.5 64.8 %all-to-all-start.7 = ((bf16[16,1,64,2048]{3,2,1,0:T(8,128)(2,1)}), bf16[16,1,64,2048]{3,2,1,0:T(8,128)(2,1)}, u32[]{:S(2)}, u32[]{:S(2)}) async-start(bf16[16,1,64,2048]{3,2,1,0:T(8,128)(2,1)} %copy.46), calls=%async_computation.7 | async-start | bytes 8388608 | tf_op jit(solution)/shard_map/all_to_all | solution.py:31
  395.2 4.6 %copy-start.2 = (bf16[16,1,64,2048]{3,0,2,1:T(8,128)(2,1)S(1)}, bf16[16,1,64,2048]{3,0,2,1:T(8,128)(2,1)}, u32[]{:S(2)}) copy-start(bf16[16,1,64,2048]{3,0,2,1:T(8,128)(2,1)} %copy.47) | copy-start | bytes 12582916
where the time goes:
time: 417 us; the launch traced here: 416 us
  waiting for transfers between devices  264 us (63%)
  local copies, waits for them, and re-layouts  69.6 us (17%)
  starting transfers between devices  61.6 us (15%)
  matrix products  12.6 us (3%)
  other arithmetic  7.58 us (2%)
    all_to_all x8, waiting for transfers between devices, cut_exchange(): lax.all_to_all(piece, axis, split_axis=0, concat_axis=0, tiled=True)  264 us
    all_to_all x8, starting transfers between devices, cut_exchange(): lax.all_to_all(piece, axis, split_axis=0, concat_axis=0, tiled=True)  61.6 us
    split x6, local copies, waits for them, and re-layouts, cut_exchange(): jnp.split(tiles, edges_of(tiles.shape[cut], pieces), axis=cut)  33.3 us
    all_to_all x4, local copies, waits for them, and re-layouts, cut_exchange(): lax.all_to_all(piece, axis, split_axis=0, concat_axis=0, tiled=True)  22.2 us
    dot_general x3, matrix products, place(): jnp.einsum('sk,krd->srd', table.astype(jnp.bfloat16), rows, preferred_ele...  12.6 us
    convert_element_type x1, local copies, waits for them, and re-layouts, place(): moved = jnp.einsum('sk,krd->srd', table.astype(jnp.bfloat16), rows, prefe...  11.4 us
  transfers between devices with their start and end apart: 8, of which 5 were waited for; matrix products, arithmetic and copies ran while one was open for 16% of the time, Pallas kernels for 0%

commit v1 on v0

v1 whole, which is shorter than its diff:
```python
import jax
import jax.numpy as jnp
from jax import lax
from jax.experimental import pallas as pl
from jax.experimental.pallas import tpu as pltpu
from jax.sharding import PartitionSpec as P


TILES_SEQ = 32
CHUNKS = (48, 32, 24, 24)
RESIDENT_ROWS = 24
SHIFT_ORDER = (4, 3, 5, 2, 6, 1, 7, 0)


ANY = pl.BlockSpec(memory_space=pl.ANY)
SMEM = pl.BlockSpec(memory_space=pltpu.SMEM)
VMEM = pl.BlockSpec(memory_space=pltpu.VMEM)


def each(count, fn):
    lax.fori_loop(0, count, lambda i, carry: (fn(i), carry)[1], 0)


def shift_order(depth):
    pairs = depth // 2
    return SHIFT_ORDER if pairs == 8 else tuple(range(1, pairs)) + (0,)


def shift_pairs(depth, shift):
    return [(i, (i + 2 * shift) % depth) for i in range(depth)]


def label_first(dest, key, depth):
    def kernel(dest_ref, key_ref, out_ref):
        def clear(s):
            out_ref[s, 0, 0] = -1

        each(depth, clear)

        def note(t):
            peer = lax.rem(dest_ref[t], depth)
            out_ref[peer, 0, 0] = dest_ref[t]
            out_ref[peer, 0, 1] = key_ref[t]

        each(dest.shape[0], note)

    return pl.pallas_call(
        kernel,
        in_specs=[SMEM, SMEM],
        out_specs=SMEM,
        out_shape=jax.ShapeDtypeStruct((depth, 1, 128), jnp.int32),
    )(dest, key)


def label_second(meta, depth, groups):
    def kernel(meta_ref, out_ref):
        def clear(g):
            out_ref[g, 0, 0] = -1

        each(groups, clear)

        def note(h):
            @pl.when(meta_ref[h, 0, 0] >= 0)
            def _():
                out_ref[meta_ref[h, 0, 0] // depth, 0, 0] = meta_ref[h, 0, 1]

        each(depth, note)

    return pl.pallas_call(
        kernel,
        in_specs=[SMEM],
        out_specs=SMEM,
        out_shape=jax.ShapeDtypeStruct((groups, 1, 128), jnp.int32),
    )(meta)


def pack_first(embeds, twin, dest, twin_dest, lengths, gain, start, rows, depth, groups_y):
    tiles, tile_rows, width = embeds.shape
    order = shift_order(depth)
    pairs = depth // 2

    def kernel(dest_ref, twin_dest_ref, len_ref, x_ref, twin_ref, gain_ref, *rest):
        outs = rest[:pairs]
        xin, y, source, sem_in, sem_out = rest[pairs:]
        gz = lax.axis_index("gz")
        core = lax.rem(gz, 2)
        chip = gz // 2
        group = lax.axis_index("gx") * groups_y + lax.axis_index("gy")

        def clear(s):
            source[s] = -1

        each(depth, clear)

        def copy_in(refs, t, slot):
            return pltpu.make_async_copy(
                refs.at[t, pl.ds(start, rows)], xin.at[slot], sem_in.at[slot]
            )

        def note(dests, refs, from_core):
            def one(t):
                peer = lax.rem(dests[t], depth)

                @pl.when(lax.rem(peer, 2) == core)
                def _():
                    slot = lax.rem(peer // 2 - chip + pairs, pairs) * 2 + from_core
                    source[slot] = t
                    copy_in(refs, t, slot).start()

            each(tiles, one)

        note(dest_ref, x_ref, core)
        note(twin_dest_ref, twin_ref, 1 - core)

        def compute(slot):
            t = source[slot]

            @pl.when(t >= 0)
            def _():
                copy_in(x_ref, t, slot).wait()
                from_core = lax.rem(slot, 2)
                tile = (group * depth + chip * 2 + from_core) * tiles + t
                limit = len_ref[tile // TILES_SEQ]
                values = xin[slot].astype(jnp.float32)
                meansq = jnp.sum(values * values, axis=-1, keepdims=True) * (1.0 / width)
                scaled = values * lax.rsqrt(jnp.maximum(meansq, 0.25)) * gain_ref[...]
                row = lax.broadcasted_iota(jnp.int32, (rows, 1), 0)
                keep = lax.rem(tile, TILES_SEQ) * tile_rows + start + row < limit
                y[slot] = jnp.where(keep, scaled, 0.0).astype(y.dtype)

        each(depth, compute)

        def copy_out(s, from_core):
            slot = order[s] * 2 + from_core
            return pltpu.make_async_copy(y.at[slot], outs[s].at[from_core], sem_out.at[slot])

        where = [(s, from_core) for s in range(pairs) for from_core in range(2)]
        for s, from_core in where:
            valid = source[order[s] * 2 + from_core] >= 0
            pl.when(valid)(lambda s=s, from_core=from_core: copy_out(s, from_core).start())
        for s, from_core in where:
            valid = source[order[s] * 2 + from_core] >= 0
            pl.when(valid)(lambda s=s, from_core=from_core: copy_out(s, from_core).wait())

    return pl.pallas_call(
        kernel,
        in_specs=[SMEM, SMEM, SMEM, ANY, ANY, VMEM],
        out_specs=[ANY] * pairs,
        out_shape=[jax.ShapeDtypeStruct((2, rows, width), embeds.dtype)] * pairs,
        scratch_shapes=[
            pltpu.VMEM((depth, rows, width), embeds.dtype),
            pltpu.VMEM((depth, rows, width), embeds.dtype),
            pltpu.SMEM((depth,), jnp.int32),
            pltpu.SemaphoreType.DMA((depth,)),
            pltpu.SemaphoreType.DMA((depth,)),
        ],
    )(dest, twin_dest, lengths, embeds, twin, gain.reshape(1, width))


def pack_second(arrived, meta, depth, groups):
    _, rows, width = arrived[0].shape
    resident = rows <= RESIDENT_ROWS
    order = shift_order(depth)
    pairs = depth // 2

    def kernel(meta_ref, *rest):
        ins = rest[:pairs]
        if resident:
            out_ref, sem_out = rest[pairs:]
        else:
            out_ref, held, sem_in, sem_out = rest[pairs:]
        chip = lax.axis_index("gz") // 2

        dests = []
        for s in range(pairs):
            for from_core in range(2):
                peer = lax.rem(chip - order[s] + pairs, pairs) * 2 + from_core
                dests.append(meta_ref[peer, 0, 0])

        def inward(n):
            return pltpu.make_async_copy(ins[n // 2].at[n % 2], held.at[n], sem_in.at[n])

        def outward(n):
            here = ins[n // 2].at[n % 2] if resident else held.at[n]
            return pltpu.make_async_copy(here, out_ref.at[dests[n] // depth], sem_out.at[n])

        if not resident:
            for n in range(depth):
                pl.when(dests[n] >= 0)(lambda n=n: inward(n).start())
        for n in range(depth):

            @pl.when(dests[n] >= 0)
            def _(n=n):
                if not resident:
                    inward(n).wait()
                outward(n).start()

        for n in range(depth):
            pl.when(dests[n] >= 0)(lambda n=n: outward(n).wait())

    scratch = []
    if not resident:
        scratch = [
            pltpu.VMEM((depth, rows, width), arrived[0].dtype),
            pltpu.SemaphoreType.DMA((depth,)),
        ]
    return pl.pallas_call(
        kernel,
        in_specs=[SMEM] + [VMEM if resident else ANY] * pairs,
        out_specs=ANY,
        out_shape=jax.ShapeDtypeStruct((groups, rows, width), arrived[0].dtype),
        scratch_shapes=scratch + [pltpu.SemaphoreType.DMA((depth,))],
    )(meta, *arrived)


def unpack(arrived, meta, packed, start, tile_rows, cap):
    groups, rows, width = arrived.shape
    first = packed is None
    resident = rows <= RESIDENT_ROWS and not first

    def kernel(meta_ref, in_ref, *rest):
        if first:
            out_ref, held, sem_in, sem_out, zeros, sem_zero = rest
        elif resident:
            _, out_ref, sem_out = rest
        else:
            _, out_ref, held, sem_in, sem_out = rest
        keys = [meta_ref[g, 0, 0] for g in range(groups)]

        def inward(g):
            return pltpu.make_async_copy(in_ref.at[g], held.at[g], sem_in.at[g])

        if not resident:
            for g in range(groups):
                pl.when(keys[g] >= 0)(lambda g=g: inward(g).start())
        ranks = []
        for g in range(groups):
            rank = jnp.int32(0)
            for u in range(groups):
                if u != g:
                    rank = rank + ((keys[u] >= 0) & (keys[u] < keys[g])).astype(jnp.int32)
            ranks.append(rank)
        if first:
            count = jnp.int32(0)
            for g in range(groups):
                count = count + (keys[g] >= 0).astype(jnp.int32)
            zeros[...] = jnp.zeros(zeros.shape, zeros.dtype)

            def fill(s):
                return pltpu.make_async_copy(zeros, out_ref.at[s], sem_zero.at[s])

            each(cap, lambda s: pl.when(s >= count)(lambda: fill(s).start()))

        def outward(g):
            here = in_ref if resident else held
            return pltpu.make_async_copy(
                here.at[g], out_ref.at[ranks[g], pl.ds(start, rows)], sem_out.at[g]
            )

        for g in range(groups):

            @pl.when(keys[g] >= 0)
            def _(g=g):
                if not resident:
                    inward(g).wait()
                outward(g).start()

        for g in range(groups):
            pl.when(keys[g] >= 0)(lambda g=g: outward(g).wait())
        if first:
            each(cap, lambda s: pl.when(s >= count)(lambda: fill(s).wait()))

    scratch = [pltpu.SemaphoreType.DMA((groups,))]
    if not resident:
        scratch = [
            pltpu.VMEM((groups, rows, width), arrived.dtype),
            pltpu.SemaphoreType.DMA((groups,)),
        ] + scratch
    if first:
        scratch += [
            pltpu.VMEM((tile_rows, width), arrived.dtype),
            pltpu.SemaphoreType.DMA((cap,)),
        ]
    return pl.pallas_call(
        kernel,
        in_specs=[SMEM, VMEM if resident else ANY] + ([] if first else [ANY]),
        out_specs=ANY,
        out_shape=jax.ShapeDtypeStruct((cap, tile_rows, width), arrived.dtype),
        scratch_shapes=scratch,
        input_output_aliases={} if first else {2: 0},
    )(meta, arrived, *(() if first else (packed,)))


def shards(embeds, dest_device, shuffle_key, lengths, gain):
    tiles, tile_rows, _ = embeds.shape
    depth = lax.axis_size("gz")
    groups_y = lax.axis_size("gy")
    groups = lax.axis_size("gx") * groups_y
    chunks = CHUNKS if sum(CHUNKS) == tile_rows else (tile_rows,)
    starts = [sum(chunks[:c]) for c in range(len(chunks))]

    partner = [(i, i ^ 1) for i in range(depth)]
    twin = lax.ppermute(embeds, "gz", partner)
    twin_dest = lax.ppermute(dest_device, "gz", partner)
    meta = label_first(dest_device, shuffle_key, depth)
    meta = lax.all_to_all(meta, "gz", split_axis=0, concat_axis=0, tiled=True)
    last_meta = label_second(meta, depth, groups)
    last_meta = lax.all_to_all(
        last_meta, ("gx", "gy"), split_axis=0, concat_axis=0, tiled=True
    )
    meta, last_meta = lax.optimization_barrier((meta, last_meta))

    crossing = []
    for start, rows in zip(starts, chunks):
        sent = pack_first(
            embeds, twin, dest_device, twin_dest, lengths, gain, start, rows, depth, groups_y
        )
        crossing.append(
            [
                lax.ppermute(slots, "gz", shift_pairs(depth, shift)) if shift else slots
                for slots, shift in zip(sent, shift_order(depth))
            ]
        )

    packed = landed = None
    for c, (start, rows) in enumerate(zip(starts, chunks)):
        sent = pack_second(crossing[c], meta, depth, groups)
        if c > 0:
            sent, landed = lax.optimization_barrier((sent, landed))
            packed = unpack(
                landed, last_meta, packed, starts[c - 1], tile_rows, 2 * tiles
            )
        landed = lax.all_to_all(sent, ("gx", "gy"), split_axis=0, concat_axis=0, tiled=True)
    return unpack(landed, last_meta, packed, starts[-1], tile_rows, 2 * tiles)


def solution(mesh):
    return jax.shard_map(
        shards,
        mesh=mesh,
        in_specs=(
            P(("gx", "gy", "gz"), None, None),
            P(("gx", "gy", "gz")),
            P(("gx", "gy", "gz")),
            P(),
            P(),
        ),
        out_specs=P(("gx", "gy", "gz"), None, None),
        check_vma=False,
    )
```

time: 417 us -> 316 us (0.76)
  waiting for transfers between devices: 264 us -> 126 us
  local copies, waits for them, and re-layouts: 69.6 us -> 4.3 us
  Pallas kernels: 0 us -> 45.5 us
  starting transfers between devices: 61.6 us -> 102 us
  blocking collectives: 0 us -> 34.2 us
  matrix products: 12.6 us -> 0 us
  other arithmetic: 7.58 us -> 0 us
    all_to_all x8 -> x4, waiting for transfers between devices: 264 us -> 14 us  [shards(): lax.all_to_all(sent, ('gx', 'gy'), split_axis=0, concat_axis=0, tiled=True)]
    ppermute x0 -> x30, waiting for transfers between devices: none -> 112 us  [the longest x28 105 us: shards(): lax.ppermute(slots, 'gz', shift_pairs(depth, shift))]
    ppermute x0 -> x30, starting transfers between devices: none -> 77.8 us  [the longest x28 77.3 us: shards(): lax.ppermute(slots, 'gz', shift_pairs(depth, shift))]
    pallas_call x0 -> x14, Pallas kernels: none -> 45.5 us  [the longest x4 18.2 us: pack_first(): pl.pallas_call(kernel, in_specs=[SMEM, SMEM, SMEM, ANY, ANY, VMEM], out_s...]
    all_to_all x8 -> x4, starting transfers between devices: 61.6 us -> 24.4 us  [shards(): lax.all_to_all(sent, ('gx', 'gy'), split_axis=0, concat_axis=0, tiled=True)]
    all_to_all x0 -> x2, blocking collectives: none -> 34.2 us  [the longest x1 19.4 us: shards(): meta = lax.all_to_all(meta, 'gz', split_axis=0, concat_axis=0, tiled=True)]
    split x6 -> x0, local copies, waits for them, and re-layouts: 33.3 us -> none  [cut_exchange(): jnp.split(tiles, edges_of(tiles.shape[cut], pieces), axis=cut)]
    all_to_all x4 -> x0, local copies, waits for them, and re-layouts: 22.2 us -> none  [cut_exchange(): lax.all_to_all(piece, axis, split_axis=0, concat_axis=0, tiled=True)]
  transfers between devices with their start and end apart: 8 -> 34, of which waited for: 5 -> 23; matrix products, arithmetic and copies ran while one was open for 16% -> 0% of each run, Pallas kernels for 0% -> 11%
where the time goes in v1:
time: 316 us; the launch traced here: 313 us
  waiting for transfers between devices  126 us (40%)
  starting transfers between devices  102 us (32%)
  Pallas kernels  45.5 us (14%)
  blocking collectives  34.2 us (11%)
  local copies, waits for them, and re-layouts  4.3 us (1%)
    ppermute x28, waiting for transfers between devices, shards(): lax.ppermute(slots, 'gz', shift_pairs(depth, shift))  105 us
    ppermute x28, starting transfers between devices, shards(): lax.ppermute(slots, 'gz', shift_pairs(depth, shift))  77.3 us
    all_to_all x4, starting transfers between devices, shards(): lax.all_to_all(sent, ('gx', 'gy'), split_axis=0, concat_axis=0, tiled=True)  24.4 us
    all_to_all x1, blocking collectives, shards(): meta = lax.all_to_all(meta, 'gz', split_axis=0, concat_axis=0, tiled=True)  19.4 us
    pallas_call x4, Pallas kernels, pack_first(): pl.pallas_call(kernel, in_specs=[SMEM, SMEM, SMEM, ANY, ANY, VMEM], out_s...  18.2 us
    all_to_all x1, blocking collectives, shards(): lax.all_to_all(last_meta, ('gx', 'gy'), split_axis=0, concat_axis=0, tile...  14.8 us
    all_to_all x4, waiting for transfers between devices, shards(): lax.all_to_all(sent, ('gx', 'gy'), split_axis=0, concat_axis=0, tiled=True)  14 us
    pallas_call x4, Pallas kernels, unpack(): pl.pallas_call(kernel, in_specs=[SMEM, VMEM if resident else ANY] + ([] i...  12.6 us
  transfers between devices with their start and end apart: 34, of which 23 were waited for; matrix products, arithmetic and copies ran while one was open for 0% of the time, Pallas kernels for 11%

profile of v1, /device:TPU:32, one launch (start us, length us, event | category | flops | bytes accessed | tf_op | source)
XLA Modules:
  0.0 313.2 jit_solution(8981675049434578148)
XLA Ops:
  0.5 7.0 %collective-permute-done.twin_dest_ref = s32[8]{0:T(128)S(1)} collective-permute-done((s32[8]{0:T(128)}, s32[8]{0:T(128)S(1)}, u32[]{:S(2)}, u32[]{:S(2)}) %collective-permute-start) | collective-permute-done | bytes 64 | tf_op jit(solution)/shard_map/ppermute | solution.py:304
  8.1 5.0 %shard_map.63 = (bf16[2,48,2048]{2,1,0:T(8,128)(2,1)}, bf16[2,48,2048]{2,1,0:T(8,128)(2,1)}, bf16[2,48,2048]{2,1,0:T(8,128)(2,1)}, bf16[2,48,2048]{2,1,0:T(8,128...) custom-call(s32[8]{0:T(128)} %dest_ref.9, ...), custom_call_target="tpu_custom_call" | custom-call | tf_op jit(solution)/shard_map/pallas_call | solution.py:145
  13.1 6.0 %collective-permute-start.23 = (bf16[2,48,2048]{2,1,0:T(8,128)(2,1)}, bf16[2,48,2048]{2,1,0:T(8,128)(2,1)S(1)}, u32[]{:S(2)}, u32[]{:S(2)}) collective-permute-start(bf16[2,48,2048]{2,1,0:T(8,128)(2,1)} %get-tuple-element.71), channel_id=1, source_target_pairs={{0,8},{1,9},{2,10},{3,11},{4,12},{5,13},{6,14},{7,15},{8,0},{9,1},... | collective-permute-start | bytes 1179656 | tf_op jit(solution)/shard_map/ppermute | solution.py:320
  19.4 4.7 %collective-permute-start.25 = (bf16[2,48,2048]{2,1,0:T(8,128)(2,1)}, bf16[2,48,2048]{2,1,0:T(8,128)(2,1)S(1)}, u32[]{:S(2)}, u32[]{:S(2)}) collective-permute-start(bf16[2,48,2048]{2,1,0:T(8,128)(2,1)} %get-tuple-element.73), channel_id=1, source_target_pairs={{0,10},{1,11},{2,12},{3,13},{4,14},{5,15},{6,0},{7,1},{8,2},{9,3},... | collective-permute-start | bytes 1179656 | tf_op jit(solution)/shard_map/ppermute | solution.py:320
  24.6 3.7 %collective-permute-start.27 = (bf16[2,48,2048]{2,1,0:T(8,128)(2,1)}, bf16[2,48,2048]{2,1,0:T(8,128)(2,1)S(1)}, u32[]{:S(2)}, u32[]{:S(2)}) collective-permute-start(bf16[2,48,2048]{2,1,0:T(8,128)(2,1)} %get-tuple-element.75), channel_id=1, source_target_pairs={{0,12},{1,13},{2,14},{3,15},{4,0},{5,1},{6,2},{7,3},{8,4},{9,5},{1... | collective-permute-start | bytes 1179656 | tf_op jit(solution)/shard_map/ppermute | solution.py:320
  28.2 12.5 %collective-permute-done.23.rest_0_ = bf16[2,48,2048]{2,1,0:T(8,128)(2,1)S(1)} collective-permute-done((bf16[2,48,2048]{2,1,0:T(8,128)(2,1)}, bf16[2,48,2048]{2,1,0:T(8,128)(2,1)S(1)}, u32[]{:S(2)}, u32[]{:S(2)}) %collective-permute-start.23) | collective-permute-done | bytes 393248 | tf_op jit(solution)/shard_map/ppermute | solution.py:320
  43.1 19.9 %collective-permute-done.24.rest_1_ = bf16[2,48,2048]{2,1,0:T(8,128)(2,1)S(1)} collective-permute-done((bf16[2,48,2048]{2,1,0:T(8,128)(2,1)}, bf16[2,48,2048]{2,1,0:T(8,128)(2,1)S(1)}, u32[]{:S(2)}, u32[]{:S(2)}) %collective-permute-start.24) | collective-permute-done | bytes 393248 | tf_op jit(solution)/shard_map/ppermute | solution.py:320
  63.0 4.5 %collective-permute-start.29 = (bf16[2,48,2048]{2,1,0:T(8,128)(2,1)}, bf16[2,48,2048]{2,1,0:T(8,128)(2,1)S(1)}, u32[]{:S(2)}, u32[]{:S(2)}) collective-permute-start(bf16[2,48,2048]{2,1,0:T(8,128)(2,1)} %get-tuple-element.77), channel_id=1, source_target_pairs={{0,14},{1,15},{2,0},{3,1},{4,2},{5,3},{6,4},{7,5},{8,6},{9,7},{10,... | collective-permute-start | bytes 1179656 | tf_op jit(solution)/shard_map/ppermute | solution.py:320
  69.0 19.4 %all_to_all.30.meta_ref = s32[16,1,128]{2,1,0:T(1,128)} all-to-all(s32[16,1,128]{2,1,0:T(1,128)} %shard_map.55), channel_id=1, replica_groups=mesh['gx'=4,'gy'=4,'gz'=16] {'gz'}, dimensions={0} | all-to-all | bytes 16384 | tf_op jit(solution)/shard_map/all_to_all | solution.py:306
  90.2 14.8 %all_to_all.31.meta_ref = s32[16,1,128]{2,1,0:T(1,128)} all-to-all(s32[16,1,128]{2,1,0:T(1,128)} %shard_map.56), channel_id=1, replica_groups=mesh['gx'=4,'gy'=4,'gz'=16] {'gx','gy'}, dimensions={0} | all-to-all | bytes 16384 | tf_op jit(solution)/shard_map/all_to_all | solution.py:308
  106.3 3.2 %shard_map.64 = bf16[16,48,2048]{2,1,0:T(8,128)(2,1)} custom-call(s32[16,1,128]{2,1,0:T(1,128)} %all_to_all.30.meta_ref, bf16[2,48,2048]{2,1,0:T(8,128)(2,1)} %copy-done.3, bf16[2,48,2048]{2,1,0:T(8,128)(2,1)} %copy-done.4, bf16[2,48,2048]{2,1,0:T(8,128)(2,1)} %copy-done.5, bf16[2,48,2048]{2,1,0:T(8,128)(2,1)} %copy-done.6, bf16[2,48,2048]{2,1,0:T(8,128)(2,1)} %copy-done.7, ...), custom_call_target="tpu_custom_call" | custom-call | tf_op jit(solution)/shard_map/pallas_call | solution.py:207
  109.6 3.8 %all-to-all-start.2 = ((bf16[16,48,2048]{2,1,0:T(8,128)(2,1)}), bf16[16,48,2048]{2,1,0:T(8,128)(2,1)S(1)}, u32[]{:S(2)}, u32[]{:S(2)}) async-start(bf16[16,48,2048]{2,1,0:T(8,128)(2,1)} %shard_map.64), calls=%async_computation.2 | async-start | bytes 6291456 | tf_op jit(solution)/shard_map/all_to_all | solution.py:333
  113.4 4.6 %shard_map.61 = (bf16[2,32,2048]{2,1,0:T(8,128)(2,1)}, bf16[2,32,2048]{2,1,0:T(8,128)(2,1)}, bf16[2,32,2048]{2,1,0:T(8,128)(2,1)}, bf16[2,32,2048]{2,1,0:T(8,128...) custom-call(s32[8]{0:T(128)} %dest_ref.9, ...), custom_call_target="tpu_custom_call" | custom-call | tf_op jit(solution)/shard_map/pallas_call | solution.py:145
  118.0 5.5 %collective-permute-start.16 = (bf16[2,32,2048]{2,1,0:T(8,128)(2,1)}, bf16[2,32,2048]{2,1,0:T(8,128)(2,1)S(1)}, u32[]{:S(2)}, u32[]{:S(2)}) collective-permute-start(bf16[2,32,2048]{2,1,0:T(8,128)(2,1)} %get-tuple-element.63), channel_id=1, source_target_pairs={{0,8},{1,9},{2,10},{3,11},{4,12},{5,13},{6,14},{7,15},{8,0},{9,1},... | collective-permute-start | bytes 786440 | tf_op jit(solution)/shard_map/ppermute | solution.py:320
  124.3 4.2 %collective-permute-start.18 = (bf16[2,32,2048]{2,1,0:T(8,128)(2,1)}, bf16[2,32,2048]{2,1,0:T(8,128)(2,1)}, u32[]{:S(2)}, u32[]{:S(2)}) collective-permute-start(bf16[2,32,2048]{2,1,0:T(8,128)(2,1)} %get-tuple-element.65), channel_id=1, source_target_pairs={{0,10},{1,11},{2,12},{3,13},{4,14},{5,15},{6,0},{7,1},{8,2},{9,3},... | collective-permute-start | bytes 786440 | tf_op jit(solution)/shard_map/ppermute | solution.py:320
  128.5 4.1 %collective-permute-start.20 = (bf16[2,32,2048]{2,1,0:T(8,128)(2,1)}, bf16[2,32,2048]{2,1,0:T(8,128)(2,1)}, u32[]{:S(2)}, u32[]{:S(2)}) collective-permute-start(bf16[2,32,2048]{2,1,0:T(8,128)(2,1)} %get-tuple-element.67), channel_id=1, source_target_pairs={{0,12},{1,13},{2,14},{3,15},{4,0},{5,1},{6,2},{7,3},{8,4},{9,5},{1... | collective-permute-start | bytes 786440 | tf_op jit(solution)/shard_map/ppermute | solution.py:320
  132.6 8.3 %collective-permute-done.16.rest_0_ = bf16[2,32,2048]{2,1,0:T(8,128)(2,1)S(1)} collective-permute-done((bf16[2,32,2048]{2,1,0:T(8,128)(2,1)}, bf16[2,32,2048]{2,1,0:T(8,128)(2,1)S(1)}, u32[]{:S(2)}, u32[]{:S(2)}) %collective-permute-start.16) | collective-permute-done | bytes 262176 | tf_op jit(solution)/shard_map/ppermute | solution.py:320
  141.7 8.9 %collective-permute-done.17.rest_1_ = bf16[2,32,2048]{2,1,0:T(8,128)(2,1)} collective-permute-done((bf16[2,32,2048]{2,1,0:T(8,128)(2,1)}, bf16[2,32,2048]{2,1,0:T(8,128)(2,1)}, u32[]{:S(2)}, u32[]{:S(2)}) %collective-permute-start.17) | collective-permute-done | bytes 262176 | tf_op jit(solution)/shard_map/ppermute | solution.py:320
  150.5 6.5 %collective-permute-start.22 = (bf16[2,32,2048]{2,1,0:T(8,128)(2,1)}, bf16[2,32,2048]{2,1,0:T(8,128)(2,1)}, u32[]{:S(2)}, u32[]{:S(2)}) collective-permute-start(bf16[2,32,2048]{2,1,0:T(8,128)(2,1)} %get-tuple-element.69), channel_id=1, source_target_pairs={{0,14},{1,15},{2,0},{3,1},{4,2},{5,3},{6,4},{7,5},{8,6},{9,7},{10,... | collective-permute-start | bytes 786440 | tf_op jit(solution)/shard_map/ppermute | solution.py:320
  157.0 4.9 %collective-permute-done.19.rest_3_ = bf16[2,32,2048]{2,1,0:T(8,128)(2,1)} collective-permute-done((bf16[2,32,2048]{2,1,0:T(8,128)(2,1)}, bf16[2,32,2048]{2,1,0:T(8,128)(2,1)}, u32[]{:S(2)}, u32[]{:S(2)}) %collective-permute-start.19) | collective-permute-done | bytes 262176 | tf_op jit(solution)/shard_map/ppermute | solution.py:320
  162.8 5.0 %collective-permute-done.21.rest_5_ = bf16[2,32,2048]{2,1,0:T(8,128)(2,1)} collective-permute-done((bf16[2,32,2048]{2,1,0:T(8,128)(2,1)}, bf16[2,32,2048]{2,1,0:T(8,128)(2,1)}, u32[]{:S(2)}, u32[]{:S(2)}) %collective-permute-start.21) | collective-permute-done | bytes 262176 | tf_op jit(solution)/shard_map/ppermute | solution.py:320
  168.1 3.1 shard_map.62
  171.2 7.1 %all-to-all-start.3 = ((bf16[16,32,2048]{2,1,0:T(8,128)(2,1)}), bf16[16,32,2048]{2,1,0:T(8,128)(2,1)}, u32[]{:S(2)}, u32[]{:S(2)}) async-start(bf16[16,32,2048]{2,1,0:T(8,128)(2,1)} %shard_map.62), calls=%async_computation.3 | async-start | bytes 4194304 | tf_op jit(solution)/shard_map/all_to_all | solution.py:333
  178.2 4.3 %shard_map.59 = (bf16[2,24,2048]{2,1,0:T(8,128)(2,1)}, bf16[2,24,2048]{2,1,0:T(8,128)(2,1)}, bf16[2,24,2048]{2,1,0:T(8,128)(2,1)}, bf16[2,24,2048]{2,1,0:T(8,128...) custom-call(s32[8]{0:T(128)} %dest_ref.9, ...), custom_call_target="tpu_custom_call" | custom-call | tf_op jit(solution)/shard_map/pallas_call | solution.py:145
  182.5 2.5 collective-permute-start.9
  185.1 3.7 %collective-permute-start.10 = (bf16[2,24,2048]{2,1,0:T(8,128)(2,1)}, bf16[2,24,2048]{2,1,0:T(8,128)(2,1)S(1)}, u32[]{:S(2)}, u32[]{:S(2)}) collective-permute-start(bf16[2,24,2048]{2,1,0:T(8,128)(2,1)} %get-tuple-element.56), channel_id=1, source_target_pairs={{0,6},{1,7},{2,8},{3,9},{4,10},{5,11},{6,12},{7,13},{8,14},{9,15},... | collective-permute-start | bytes 589832 | tf_op jit(solution)/shard_map/ppermute | solution.py:320
  194.2 4.3 %collective-permute-done.9.rest_0_ = bf16[2,24,2048]{2,1,0:T(8,128)(2,1)S(1)} collective-permute-done((bf16[2,24,2048]{2,1,0:T(8,128)(2,1)}, bf16[2,24,2048]{2,1,0:T(8,128)(2,1)S(1)}, u32[]{:S(2)}, u32[]{:S(2)}) %collective-permute-start.9) | collective-permute-done | bytes 196640 | tf_op jit(solution)/shard_map/ppermute | solution.py:320
  198.5 3.8 %collective-permute-start.14 = (bf16[2,24,2048]{2,1,0:T(8,128)(2,1)}, bf16[2,24,2048]{2,1,0:T(8,128)(2,1)S(1)}, u32[]{:S(2)}, u32[]{:S(2)}) collective-permute-start(bf16[2,24,2048]{2,1,0:T(8,128)(2,1)} %get-tuple-element.60), channel_id=1, source_target_pairs={{0,2},{1,3},{2,4},{3,5},{4,6},{5,7},{6,8},{7,9},{8,10},{9,11},{10,... | collective-permute-start | bytes 589832 | tf_op jit(solution)/shard_map/ppermute | solution.py:320
  202.4 7.2 %collective-permute-done.10.rest_1_ = bf16[2,24,2048]{2,1,0:T(8,128)(2,1)S(1)} collective-permute-done((bf16[2,24,2048]{2,1,0:T(8,128)(2,1)}, bf16[2,24,2048]{2,1,0:T(8,128)(2,1)S(1)}, u32[]{:S(2)}, u32[]{:S(2)}) %collective-permute-start.10) | collective-permute-done | bytes 196640 | tf_op jit(solution)/shard_map/ppermute | solution.py:320
  209.6 4.6 %collective-permute-start.15 = (bf16[2,24,2048]{2,1,0:T(8,128)(2,1)}, bf16[2,24,2048]{2,1,0:T(8,128)(2,1)S(1)}, u32[]{:S(2)}, u32[]{:S(2)}) collective-permute-start(bf16[2,24,2048]{2,1,0:T(8,128)(2,1)} %get-tuple-element.61), channel_id=1, source_target_pairs={{0,14},{1,15},{2,0},{3,1},{4,2},{5,3},{6,4},{7,5},{8,6},{9,7},{10,... | collective-permute-start | bytes 589832 | tf_op jit(solution)/shard_map/ppermute | solution.py:320
  214.6 3.6 %collective-permute-done.12.rest_3_ = bf16[2,24,2048]{2,1,0:T(8,128)(2,1)S(1)} collective-permute-done((bf16[2,24,2048]{2,1,0:T(8,128)(2,1)}, bf16[2,24,2048]{2,1,0:T(8,128)(2,1)S(1)}, u32[]{:S(2)}, u32[]{:S(2)}) %collective-permute-start.12) | collective-permute-done | bytes 196640 | tf_op jit(solution)/shard_map/ppermute | solution.py:320
  218.8 3.1 collective-permute-done.14.rest_5_
  223.5 2.5 shard_map.60
  226.0 6.9 %all-to-all-start.4 = ((bf16[16,24,2048]{2,1,0:T(8,128)(2,1)}), bf16[16,24,2048]{2,1,0:T(8,128)(2,1)S(1)}, u32[]{:S(2)}, u32[]{:S(2)}) async-start(bf16[16,24,2048]{2,1,0:T(8,128)(2,1)} %shard_map.60), calls=%async_computation.4 | async-start | bytes 3145728 | tf_op jit(solution)/shard_map/all_to_all | solution.py:333
  232.9 4.3 %shard_map.57 = (bf16[2,24,2048]{2,1,0:T(8,128)(2,1)}, bf16[2,24,2048]{2,1,0:T(8,128)(2,1)}, bf16[2,24,2048]{2,1,0:T(8,128)(2,1)}, bf16[2,24,2048]{2,1,0:T(8,128...) custom-call(s32[8]{0:T(128)} %dest_ref.9, ...), custom_call_target="tpu_custom_call" | custom-call | tf_op jit(solution)/shard_map/pallas_call | solution.py:145
  238.0 4.7 %collective-permute-start.3 = (bf16[2,24,2048]{2,1,0:T(8,128)(2,1)}, bf16[2,24,2048]{2,1,0:T(8,128)(2,1)S(1)}, u32[]{:S(2)}, u32[]{:S(2)}) collective-permute-start(bf16[2,24,2048]{2,1,0:T(8,128)(2,1)} %get-tuple-element.48), channel_id=1, source_target_pairs={{0,6},{1,7},{2,8},{3,9},{4,10},{5,11},{6,12},{7,13},{8,14},{9,15},... | collective-permute-start | bytes 589832 | tf_op jit(solution)/shard_map/ppermute | solution.py:320
  244.4 2.7 collective-permute-start.6
  247.2 7.2 %collective-permute-done.2.rest_0_ = bf16[2,24,2048]{2,1,0:T(8,128)(2,1)S(1)} collective-permute-done((bf16[2,24,2048]{2,1,0:T(8,128)(2,1)}, bf16[2,24,2048]{2,1,0:T(8,128)(2,1)S(1)}, u32[]{:S(2)}, u32[]{:S(2)}) %collective-permute-start.2) | collective-permute-done | bytes 196640 | tf_op jit(solution)/shard_map/ppermute | solution.py:320
  255.2 9.9 %collective-permute-done.3.rest_1_ = bf16[2,24,2048]{2,1,0:T(8,128)(2,1)S(1)} collective-permute-done((bf16[2,24,2048]{2,1,0:T(8,128)(2,1)}, bf16[2,24,2048]{2,1,0:T(8,128)(2,1)S(1)}, u32[]{:S(2)}, u32[]{:S(2)}) %collective-permute-start.3) | collective-permute-done | bytes 196640 | tf_op jit(solution)/shard_map/ppermute | solution.py:320
  265.1 2.7 collective-permute-start.8
  268.6 3.8 %collective-permute-done.5.rest_3_ = bf16[2,24,2048]{2,1,0:T(8,128)(2,1)S(1)} collective-permute-done((bf16[2,24,2048]{2,1,0:T(8,128)(2,1)}, bf16[2,24,2048]{2,1,0:T(8,128)(2,1)S(1)}, u32[]{:S(2)}, u32[]{:S(2)}) %collective-permute-start.5) | collective-permute-done | bytes 196640 | tf_op jit(solution)/shard_map/ppermute | solution.py:320
  275.9 2.5 shard_map.58
  278.5 6.7 %all-to-all-start.5 = ((bf16[16,24,2048]{2,1,0:T(8,128)(2,1)}), bf16[16,24,2048]{2,1,0:T(8,128)(2,1)S(1)}, u32[]{:S(2)}, u32[]{:S(2)}) async-start(bf16[16,24,2048]{2,1,0:T(8,128)(2,1)} %shard_map.58), calls=%async_computation.5 | async-start | bytes 3145728 | tf_op jit(solution)/shard_map/all_to_all | solution.py:333
  285.1 4.2 %shard_map.65.rest_0_ = bf16[16,128,2048]{2,1,0:T(8,128)(2,1)} custom-call(s32[16,1,128]{2,1,0:T(1,128)} %all_to_all.31.meta_ref, bf16[16,48,2048]{2,1,0:T(8,128)(2,1)} %copy-done), custom_call_target="tpu_custom_call" | custom-call | tf_op jit(solution)/shard_map/pallas_call | solution.py:284
  289.4 3.1 shard_map.66.rest_0_
  292.5 2.7 shard_map.67.rest_0_
  295.2 14.0 %all-to-all-done.5.in_ref = bf16[16,24,2048]{2,1,0:T(8,128)(2,1)S(1)} async-done(((bf16[16,24,2048]{2,1,0:T(8,128)(2,1)}), bf16[16,24,2048]{2,1,0:T(8,128)(2,1)S(1)}, u32[]{:S(2)}, u32[]{:S(2)}) %all-to-all-start.5) | async-done | bytes 1572896 | tf_op jit(solution)/shard_map/all_to_all | solution.py:333
  310.3 2.7 shard_map.68
  (88 shorter events, 28.4 us)
Async XLA Ops:
  0.0 7.5 %collective-permute-start.1 = (bf16[8,128,2048]{2,1,0:T(8,128)(2,1)}, bf16[8,128,2048]{2,1,0:T(8,128)(2,1)}, u32[]{:S(2)}, u32[]{:S(2)}) collective-permute-start(bf16[8,128,2048]{2,1,0:T(8,128)(2,1)} %x_ref.7), channel_id=1, source_target_pairs={{0,1},{1,0},{2,3},{3,2},{4,5},{5,4},{6,7},{7,6},{8,9},{9,8},{10,11... | collective-permute-start | bytes 12582920 | tf_op jit(solution)/shard_map/ppermute | solution.py:303
  0.0 7.5 %collective-permute-start = (s32[8]{0:T(128)}, s32[8]{0:T(128)S(1)}, u32[]{:S(2)}, u32[]{:S(2)}) collective-permute-start(s32[8]{0:T(128)} %dest_ref.9), channel_id=1, source_target_pairs={{0,1},{1,0},{2,3},{3,2},{4,5},{5,4},{6,7},{7,6},{8,9},{9,8},{10,11... | collective-permute-start | bytes 104 | tf_op jit(solution)/shard_map/ppermute | solution.py:304
  13.1 27.7 %collective-permute-start.23 = (bf16[2,48,2048]{2,1,0:T(8,128)(2,1)}, bf16[2,48,2048]{2,1,0:T(8,128)(2,1)S(1)}, u32[]{:S(2)}, u32[]{:S(2)}) collective-permute-start(bf16[2,48,2048]{2,1,0:T(8,128)(2,1)} %get-tuple-element.71), channel_id=1, source_target_pairs={{0,8},{1,9},{2,10},{3,11},{4,12},{5,13},{6,14},{7,15},{8,0},{9,1},... | collective-permute-start | bytes 1179656 | tf_op jit(solution)/shard_map/ppermute | solution.py:320
  19.1 44.0 %collective-permute-start.24 = (bf16[2,48,2048]{2,1,0:T(8,128)(2,1)}, bf16[2,48,2048]{2,1,0:T(8,128)(2,1)S(1)}, u32[]{:S(2)}, u32[]{:S(2)}) collective-permute-start(bf16[2,48,2048]{2,1,0:T(8,128)(2,1)} %get-tuple-element.72), channel_id=1, source_target_pairs={{0,6},{1,7},{2,8},{3,9},{4,10},{5,11},{6,12},{7,13},{8,14},{9,15},... | collective-permute-start | bytes 1179656 | tf_op jit(solution)/shard_map/ppermute | solution.py:320
  19.4 85.7 %collective-permute-start.25 = (bf16[2,48,2048]{2,1,0:T(8,128)(2,1)}, bf16[2,48,2048]{2,1,0:T(8,128)(2,1)S(1)}, u32[]{:S(2)}, u32[]{:S(2)}) collective-permute-start(bf16[2,48,2048]{2,1,0:T(8,128)(2,1)} %get-tuple-element.73), channel_id=1, source_target_pairs={{0,10},{1,11},{2,12},{3,13},{4,14},{5,15},{6,0},{7,1},{8,2},{9,3},... | collective-permute-start | bytes 1179656 | tf_op jit(solution)/shard_map/ppermute | solution.py:320
  24.1 80.9 %collective-permute-start.26 = (bf16[2,48,2048]{2,1,0:T(8,128)(2,1)}, bf16[2,48,2048]{2,1,0:T(8,128)(2,1)S(1)}, u32[]{:S(2)}, u32[]{:S(2)}) collective-permute-start(bf16[2,48,2048]{2,1,0:T(8,128)(2,1)} %get-tuple-element.74), channel_id=1, source_target_pairs={{0,4},{1,5},{2,6},{3,7},{4,8},{5,9},{6,10},{7,11},{8,12},{9,13},{1... | collective-permute-start | bytes 1179656 | tf_op jit(solution)/shard_map/ppermute | solution.py:320
  24.6 80.5 %collective-permute-start.27 = (bf16[2,48,2048]{2,1,0:T(8,128)(2,1)}, bf16[2,48,2048]{2,1,0:T(8,128)(2,1)S(1)}, u32[]{:S(2)}, u32[]{:S(2)}) collective-permute-start(bf16[2,48,2048]{2,1,0:T(8,128)(2,1)} %get-tuple-element.75), channel_id=1, source_target_pairs={{0,12},{1,13},{2,14},{3,15},{4,0},{5,1},{6,2},{7,3},{8,4},{9,5},{1... | collective-permute-start | bytes 1179656 | tf_op jit(solution)/shard_map/ppermute | solution.py:320
  40.7 64.4 %copy-start.3 = (bf16[2,48,2048]{2,1,0:T(8,128)(2,1)}, bf16[2,48,2048]{2,1,0:T(8,128)(2,1)S(1)}, u32[]{:S(2)}) copy-start(bf16[2,48,2048]{2,1,0:T(8,128)(2,1)S(1)} %collective-permute-done.23.rest_0_) | copy-start | bytes 1179652
  40.7 64.3 %collective-permute-start.28 = (bf16[2,48,2048]{2,1,0:T(8,128)(2,1)}, bf16[2,48,2048]{2,1,0:T(8,128)(2,1)S(1)}, u32[]{:S(2)}, u32[]{:S(2)}) collective-permute-start(bf16[2,48,2048]{2,1,0:T(8,128)(2,1)} %get-tuple-element.76), channel_id=1, source_target_pairs={{0,2},{1,3},{2,4},{3,5},{4,6},{5,7},{6,8},{7,9},{8,10},{9,11},{10,... | collective-permute-start | bytes 1179656 | tf_op jit(solution)/shard_map/ppermute | solution.py:320
  63.0 42.1 %copy-start.4 = (bf16[2,48,2048]{2,1,0:T(8,128)(2,1)}, bf16[2,48,2048]{2,1,0:T(8,128)(2,1)S(1)}, u32[]{:S(2)}) copy-start(bf16[2,48,2048]{2,1,0:T(8,128)(2,1)S(1)} %collective-permute-done.24.rest_1_) | copy-start | bytes 1179652
  63.0 42.1 %collective-permute-start.29 = (bf16[2,48,2048]{2,1,0:T(8,128)(2,1)}, bf16[2,48,2048]{2,1,0:T(8,128)(2,1)S(1)}, u32[]{:S(2)}, u32[]{:S(2)}) collective-permute-start(bf16[2,48,2048]{2,1,0:T(8,128)(2,1)} %get-tuple-element.77), channel_id=1, source_target_pairs={{0,14},{1,15},{2,0},{3,1},{4,2},{5,3},{6,4},{7,5},{8,6},{9,7},{10,... | collective-permute-start | bytes 1179656 | tf_op jit(solution)/shard_map/ppermute | solution.py:320
  109.6 61.5 %all-to-all-start.2 = ((bf16[16,48,2048]{2,1,0:T(8,128)(2,1)}), bf16[16,48,2048]{2,1,0:T(8,128)(2,1)S(1)}, u32[]{:S(2)}, u32[]{:S(2)}) async-start(bf16[16,48,2048]{2,1,0:T(8,128)(2,1)} %shard_map.64), calls=%async_computation.2 | async-start | bytes 6291456 | tf_op jit(solution)/shard_map/all_to_all | solution.py:333
  118.0 23.0 %collective-permute-start.16 = (bf16[2,32,2048]{2,1,0:T(8,128)(2,1)}, bf16[2,32,2048]{2,1,0:T(8,128)(2,1)S(1)}, u32[]{:S(2)}, u32[]{:S(2)}) collective-permute-start(bf16[2,32,2048]{2,1,0:T(8,128)(2,1)} %get-tuple-element.63), channel_id=1, source_target_pairs={{0,8},{1,9},{2,10},{3,11},{4,12},{5,13},{6,14},{7,15},{8,0},{9,1},... | collective-permute-start | bytes 786440 | tf_op jit(solution)/shard_map/ppermute | solution.py:320
  123.4 27.1 %collective-permute-start.17 = (bf16[2,32,2048]{2,1,0:T(8,128)(2,1)}, bf16[2,32,2048]{2,1,0:T(8,128)(2,1)}, u32[]{:S(2)}, u32[]{:S(2)}) collective-permute-start(bf16[2,32,2048]{2,1,0:T(8,128)(2,1)} %get-tuple-element.64), channel_id=1, source_target_pairs={{0,6},{1,7},{2,8},{3,9},{4,10},{5,11},{6,12},{7,13},{8,14},{9,15},... | collective-permute-start | bytes 786440 | tf_op jit(solution)/shard_map/ppermute | solution.py:320
  124.3 32.7 %collective-permute-start.18 = (bf16[2,32,2048]{2,1,0:T(8,128)(2,1)}, bf16[2,32,2048]{2,1,0:T(8,128)(2,1)}, u32[]{:S(2)}, u32[]{:S(2)}) collective-permute-start(bf16[2,32,2048]{2,1,0:T(8,128)(2,1)} %get-tuple-element.65), channel_id=1, source_target_pairs={{0,10},{1,11},{2,12},{3,13},{4,14},{5,15},{6,0},{7,1},{8,2},{9,3},... | collective-permute-start | bytes 786440 | tf_op jit(solution)/shard_map/ppermute | solution.py:320
  128.5 33.4 %collective-permute-start.19 = (bf16[2,32,2048]{2,1,0:T(8,128)(2,1)}, bf16[2,32,2048]{2,1,0:T(8,128)(2,1)}, u32[]{:S(2)}, u32[]{:S(2)}) collective-permute-start(bf16[2,32,2048]{2,1,0:T(8,128)(2,1)} %get-tuple-element.66), channel_id=1, source_target_pairs={{0,4},{1,5},{2,6},{3,7},{4,8},{5,9},{6,10},{7,11},{8,12},{9,13},{1... | collective-permute-start | bytes 786440 | tf_op jit(solution)/shard_map/ppermute | solution.py:320
  128.5 34.3 %collective-permute-start.20 = (bf16[2,32,2048]{2,1,0:T(8,128)(2,1)}, bf16[2,32,2048]{2,1,0:T(8,128)(2,1)}, u32[]{:S(2)}, u32[]{:S(2)}) collective-permute-start(bf16[2,32,2048]{2,1,0:T(8,128)(2,1)} %get-tuple-element.67), channel_id=1, source_target_pairs={{0,12},{1,13},{2,14},{3,15},{4,0},{5,1},{6,2},{7,3},{8,4},{9,5},{1... | collective-permute-start | bytes 786440 | tf_op jit(solution)/shard_map/ppermute | solution.py:320
  141.0 27.1 %copy-start.10 = (bf16[2,32,2048]{2,1,0:T(8,128)(2,1)}, bf16[2,32,2048]{2,1,0:T(8,128)(2,1)S(1)}, u32[]{:S(2)}) copy-start(bf16[2,32,2048]{2,1,0:T(8,128)(2,1)S(1)} %collective-permute-done.16.rest_0_) | copy-start | bytes 786436
  141.0 26.9 %collective-permute-start.21 = (bf16[2,32,2048]{2,1,0:T(8,128)(2,1)}, bf16[2,32,2048]{2,1,0:T(8,128)(2,1)}, u32[]{:S(2)}, u32[]{:S(2)}) collective-permute-start(bf16[2,32,2048]{2,1,0:T(8,128)(2,1)} %get-tuple-element.68), channel_id=1, source_target_pairs={{0,2},{1,3},{2,4},{3,5},{4,6},{5,7},{6,8},{7,9},{8,10},{9,11},{10,... | collective-permute-start | bytes 786440 | tf_op jit(solution)/shard_map/ppermute | solution.py:320
  150.5 17.5 %collective-permute-start.22 = (bf16[2,32,2048]{2,1,0:T(8,128)(2,1)}, bf16[2,32,2048]{2,1,0:T(8,128)(2,1)}, u32[]{:S(2)}, u32[]{:S(2)}) collective-permute-start(bf16[2,32,2048]{2,1,0:T(8,128)(2,1)} %get-tuple-element.69), channel_id=1, source_target_pairs={{0,14},{1,15},{2,0},{3,1},{4,2},{5,3},{6,4},{7,5},{8,6},{9,7},{10,... | collective-permute-start | bytes 786440 | tf_op jit(solution)/shard_map/ppermute | solution.py:320
  171.1 11.4 %copy-start = (bf16[16,48,2048]{2,1,0:T(8,128)(2,1)}, bf16[16,48,2048]{2,1,0:T(8,128)(2,1)S(1)}, u32[]{:S(2)}) copy-start(bf16[16,48,2048]{2,1,0:T(8,128)(2,1)S(1)} %all-to-all-done.2.in_ref) | copy-start | bytes 9437188
  171.2 54.8 %all-to-all-start.3 = ((bf16[16,32,2048]{2,1,0:T(8,128)(2,1)}), bf16[16,32,2048]{2,1,0:T(8,128)(2,1)}, u32[]{:S(2)}, u32[]{:S(2)}) async-start(bf16[16,32,2048]{2,1,0:T(8,128)(2,1)} %shard_map.62), calls=%async_computation.3 | async-start | bytes 4194304 | tf_op jit(solution)/shard_map/all_to_all | solution.py:333
  182.5 16.0 %collective-permute-start.9 = (bf16[2,24,2048]{2,1,0:T(8,128)(2,1)}, bf16[2,24,2048]{2,1,0:T(8,128)(2,1)S(1)}, u32[]{:S(2)}, u32[]{:S(2)}) collective-permute-start(bf16[2,24,2048]{2,1,0:T(8,128)(2,1)} %get-tuple-element.55), channel_id=1, source_target_pairs={{0,8},{1,9},{2,10},{3,11},{4,12},{5,13},{6,14},{7,15},{8,0},{9,1},... | collective-permute-start | bytes 589832 | tf_op jit(solution)/shard_map/ppermute | solution.py:320
  185.1 24.5 %collective-permute-start.10 = (bf16[2,24,2048]{2,1,0:T(8,128)(2,1)}, bf16[2,24,2048]{2,1,0:T(8,128)(2,1)S(1)}, u32[]{:S(2)}, u32[]{:S(2)}) collective-permute-start(bf16[2,24,2048]{2,1,0:T(8,128)(2,1)} %get-tuple-element.56), channel_id=1, source_target_pairs={{0,6},{1,7},{2,8},{3,9},{4,10},{5,11},{6,12},{7,13},{8,14},{9,15},... | collective-permute-start | bytes 589832 | tf_op jit(solution)/shard_map/ppermute | solution.py:320
  188.8 25.8 %collective-permute-start.11 = (bf16[2,24,2048]{2,1,0:T(8,128)(2,1)}, bf16[2,24,2048]{2,1,0:T(8,128)(2,1)S(1)}, u32[]{:S(2)}, u32[]{:S(2)}) collective-permute-start(bf16[2,24,2048]{2,1,0:T(8,128)(2,1)} %get-tuple-element.57), channel_id=1, source_target_pairs={{0,10},{1,11},{2,12},{3,13},{4,14},{5,15},{6,0},{7,1},{8,2},{9,3},... | collective-permute-start | bytes 589832 | tf_op jit(solution)/shard_map/ppermute | solution.py:320
  190.1 28.1 %collective-permute-start.12 = (bf16[2,24,2048]{2,1,0:T(8,128)(2,1)}, bf16[2,24,2048]{2,1,0:T(8,128)(2,1)S(1)}, u32[]{:S(2)}, u32[]{:S(2)}) collective-permute-start(bf16[2,24,2048]{2,1,0:T(8,128)(2,1)} %get-tuple-element.58), channel_id=1, source_target_pairs={{0,4},{1,5},{2,6},{3,7},{4,8},{5,9},{6,10},{7,11},{8,12},{9,13},{1... | collective-permute-start | bytes 589832 | tf_op jit(solution)/shard_map/ppermute | solution.py:320
  192.5 26.2 %collective-permute-start.13 = (bf16[2,24,2048]{2,1,0:T(8,128)(2,1)}, bf16[2,24,2048]{2,1,0:T(8,128)(2,1)S(1)}, u32[]{:S(2)}, u32[]{:S(2)}) collective-permute-start(bf16[2,24,2048]{2,1,0:T(8,128)(2,1)} %get-tuple-element.59), channel_id=1, source_target_pairs={{0,12},{1,13},{2,14},{3,15},{4,0},{5,1},{6,2},{7,3},{8,4},{9,5},{1... | collective-permute-start | bytes 589832 | tf_op jit(solution)/shard_map/ppermute | solution.py:320
  198.5 24.2 %copy-start.12 = (bf16[2,24,2048]{2,1,0:T(8,128)(2,1)}, bf16[2,24,2048]{2,1,0:T(8,128)(2,1)S(1)}, u32[]{:S(2)}) copy-start(bf16[2,24,2048]{2,1,0:T(8,128)(2,1)S(1)} %collective-permute-done.9.rest_0_) | copy-start | bytes 589828
  198.5 23.3 %collective-permute-start.14 = (bf16[2,24,2048]{2,1,0:T(8,128)(2,1)}, bf16[2,24,2048]{2,1,0:T(8,128)(2,1)S(1)}, u32[]{:S(2)}, u32[]{:S(2)}) collective-permute-start(bf16[2,24,2048]{2,1,0:T(8,128)(2,1)} %get-tuple-element.60), channel_id=1, source_target_pairs={{0,2},{1,3},{2,4},{3,5},{4,6},{5,7},{6,8},{7,9},{8,10},{9,11},{10,... | collective-permute-start | bytes 589832 | tf_op jit(solution)/shard_map/ppermute | solution.py:320
  209.6 13.2 %copy-start.14 = (bf16[2,24,2048]{2,1,0:T(8,128)(2,1)}, bf16[2,24,2048]{2,1,0:T(8,128)(2,1)S(1)}, u32[]{:S(2)}) copy-start(bf16[2,24,2048]{2,1,0:T(8,128)(2,1)S(1)} %collective-permute-done.10.rest_1_) | copy-start | bytes 589828
  209.6 13.2 %collective-permute-start.15 = (bf16[2,24,2048]{2,1,0:T(8,128)(2,1)}, bf16[2,24,2048]{2,1,0:T(8,128)(2,1)S(1)}, u32[]{:S(2)}, u32[]{:S(2)}) collective-permute-start(bf16[2,24,2048]{2,1,0:T(8,128)(2,1)} %get-tuple-element.61), channel_id=1, source_target_pairs={{0,14},{1,15},{2,0},{3,1},{4,2},{5,3},{6,4},{7,5},{8,6},{9,7},{10,... | collective-permute-start | bytes 589832 | tf_op jit(solution)/shard_map/ppermute | solution.py:320
  214.6 8.2 %copy-start.16 = (bf16[2,24,2048]{2,1,0:T(8,128)(2,1)}, bf16[2,24,2048]{2,1,0:T(8,128)(2,1)S(1)}, u32[]{:S(2)}) copy-start(bf16[2,24,2048]{2,1,0:T(8,128)(2,1)S(1)} %collective-permute-done.11.rest_2_) | copy-start | bytes 589828
  218.2 4.6 %copy-start.18 = (bf16[2,24,2048]{2,1,0:T(8,128)(2,1)}, bf16[2,24,2048]{2,1,0:T(8,128)(2,1)S(1)}, u32[]{:S(2)}) copy-start(bf16[2,24,2048]{2,1,0:T(8,128)(2,1)S(1)} %collective-permute-done.12.rest_3_) | copy-start | bytes 589828
  218.7 4.0 %copy-start.20 = (bf16[2,24,2048]{2,1,0:T(8,128)(2,1)}, bf16[2,24,2048]{2,1,0:T(8,128)(2,1)S(1)}, u32[]{:S(2)}) copy-start(bf16[2,24,2048]{2,1,0:T(8,128)(2,1)S(1)} %collective-permute-done.13.rest_4_) | copy-start | bytes 589828
  226.0 52.5 %all-to-all-start.4 = ((bf16[16,24,2048]{2,1,0:T(8,128)(2,1)}), bf16[16,24,2048]{2,1,0:T(8,128)(2,1)S(1)}, u32[]{:S(2)}, u32[]{:S(2)}) async-start(bf16[16,24,2048]{2,1,0:T(8,128)(2,1)} %shard_map.60), calls=%async_computation.4 | async-start | bytes 3145728 | tf_op jit(solution)/shard_map/all_to_all | solution.py:333
  237.2 17.2 %collective-permute-start.2 = (bf16[2,24,2048]{2,1,0:T(8,128)(2,1)}, bf16[2,24,2048]{2,1,0:T(8,128)(2,1)S(1)}, u32[]{:S(2)}, u32[]{:S(2)}) collective-permute-start(bf16[2,24,2048]{2,1,0:T(8,128)(2,1)} %get-tuple-element.47), channel_id=1, source_target_pairs={{0,8},{1,9},{2,10},{3,11},{4,12},{5,13},{6,14},{7,15},{8,0},{9,1},... | collective-permute-start | bytes 589832 | tf_op jit(solution)/shard_map/ppermute | solution.py:320
  238.0 27.0 %collective-permute-start.3 = (bf16[2,24,2048]{2,1,0:T(8,128)(2,1)}, bf16[2,24,2048]{2,1,0:T(8,128)(2,1)S(1)}, u32[]{:S(2)}, u32[]{:S(2)}) collective-permute-start(bf16[2,24,2048]{2,1,0:T(8,128)(2,1)} %get-tuple-element.48), channel_id=1, source_target_pairs={{0,6},{1,7},{2,8},{3,9},{4,10},{5,11},{6,12},{7,13},{8,14},{9,15},... | collective-permute-start | bytes 589832 | tf_op jit(solution)/shard_map/ppermute | solution.py:320
  242.7 25.9 %collective-permute-start.4 = (bf16[2,24,2048]{2,1,0:T(8,128)(2,1)}, bf16[2,24,2048]{2,1,0:T(8,128)(2,1)S(1)}, u32[]{:S(2)}, u32[]{:S(2)}) collective-permute-start(bf16[2,24,2048]{2,1,0:T(8,128)(2,1)} %get-tuple-element.49), channel_id=1, source_target_pairs={{0,10},{1,11},{2,12},{3,13},{4,14},{5,15},{6,0},{7,1},{8,2},{9,3},... | collective-permute-start | bytes 589832 | tf_op jit(solution)/shard_map/ppermute | solution.py:320
  243.0 29.4 %collective-permute-start.5 = (bf16[2,24,2048]{2,1,0:T(8,128)(2,1)}, bf16[2,24,2048]{2,1,0:T(8,128)(2,1)S(1)}, u32[]{:S(2)}, u32[]{:S(2)}) collective-permute-start(bf16[2,24,2048]{2,1,0:T(8,128)(2,1)} %get-tuple-element.50), channel_id=1, source_target_pairs={{0,4},{1,5},{2,6},{3,7},{4,8},{5,9},{6,10},{7,11},{8,12},{9,13},{1... | collective-permute-start | bytes 589832 | tf_op jit(solution)/shard_map/ppermute | solution.py:320
  244.4 28.0 %collective-permute-start.6 = (bf16[2,24,2048]{2,1,0:T(8,128)(2,1)}, bf16[2,24,2048]{2,1,0:T(8,128)(2,1)S(1)}, u32[]{:S(2)}, u32[]{:S(2)}) collective-permute-start(bf16[2,24,2048]{2,1,0:T(8,128)(2,1)} %get-tuple-element.51), channel_id=1, source_target_pairs={{0,12},{1,13},{2,14},{3,15},{4,0},{5,1},{6,2},{7,3},{8,4},{9,5},{1... | collective-permute-start | bytes 589832 | tf_op jit(solution)/shard_map/ppermute | solution.py:320
  254.4 20.8 %copy-start.11 = (bf16[2,24,2048]{2,1,0:T(8,128)(2,1)}, bf16[2,24,2048]{2,1,0:T(8,128)(2,1)S(1)}, u32[]{:S(2)}) copy-start(bf16[2,24,2048]{2,1,0:T(8,128)(2,1)S(1)} %collective-permute-done.2.rest_0_) | copy-start | bytes 589828
  254.4 20.3 %collective-permute-start.7 = (bf16[2,24,2048]{2,1,0:T(8,128)(2,1)}, bf16[2,24,2048]{2,1,0:T(8,128)(2,1)S(1)}, u32[]{:S(2)}, u32[]{:S(2)}) collective-permute-start(bf16[2,24,2048]{2,1,0:T(8,128)(2,1)} %get-tuple-element.52), channel_id=1, source_target_pairs={{0,2},{1,3},{2,4},{3,5},{4,6},{5,7},{6,8},{7,9},{8,10},{9,11},{10,... | collective-permute-start | bytes 589832 | tf_op jit(solution)/shard_map/ppermute | solution.py:320
  265.0 10.2 %copy-start.13 = (bf16[2,24,2048]{2,1,0:T(8,128)(2,1)}, bf16[2,24,2048]{2,1,0:T(8,128)(2,1)S(1)}, u32[]{:S(2)}) copy-start(bf16[2,24,2048]{2,1,0:T(8,128)(2,1)S(1)} %collective-permute-done.3.rest_1_) | copy-start | bytes 589828
  265.1 10.2 %collective-permute-start.8 = (bf16[2,24,2048]{2,1,0:T(8,128)(2,1)}, bf16[2,24,2048]{2,1,0:T(8,128)(2,1)S(1)}, u32[]{:S(2)}, u32[]{:S(2)}) collective-permute-start(bf16[2,24,2048]{2,1,0:T(8,128)(2,1)} %get-tuple-element.53), channel_id=1, source_target_pairs={{0,14},{1,15},{2,0},{3,1},{4,2},{5,3},{6,4},{7,5},{8,6},{9,7},{10,... | collective-permute-start | bytes 589832 | tf_op jit(solution)/shard_map/ppermute | solution.py:320
  268.6 6.6 %copy-start.15 = (bf16[2,24,2048]{2,1,0:T(8,128)(2,1)}, bf16[2,24,2048]{2,1,0:T(8,128)(2,1)S(1)}, u32[]{:S(2)}) copy-start(bf16[2,24,2048]{2,1,0:T(8,128)(2,1)S(1)} %collective-permute-done.4.rest_2_) | copy-start | bytes 589828
  272.4 2.9 copy-start.19
  278.5 10.9 %copy-start.1 = (bf16[16,24,2048]{2,1,0:T(8,128)(2,1)}, bf16[16,24,2048]{2,1,0:T(8,128)(2,1)S(1)}, u32[]{:S(2)}) copy-start(bf16[16,24,2048]{2,1,0:T(8,128)(2,1)S(1)} %all-to-all-done.4.in_ref) | copy-start | bytes 4718596
  278.5 30.7 %all-to-all-start.5 = ((bf16[16,24,2048]{2,1,0:T(8,128)(2,1)}), bf16[16,24,2048]{2,1,0:T(8,128)(2,1)S(1)}, u32[]{:S(2)}, u32[]{:S(2)}) async-start(bf16[16,24,2048]{2,1,0:T(8,128)(2,1)} %shard_map.58), calls=%async_computation.5 | async-start | bytes 3145728 | tf_op jit(solution)/shard_map/all_to_all | solution.py:333
  (12 other events, 12.6 us)

commit v2 on v1

--- a/solution.py
+++ b/solution.py
@@ -7,8 +7,7 @@
 
 
 TILES_SEQ = 32
-CHUNKS = (48, 32, 24, 24)
-RESIDENT_ROWS = 24
+CHUNKS = (56, 32, 24, 16)
 SHIFT_ORDER = (4, 3, 5, 2, 6, 1, 7, 0)
 
 
@@ -74,14 +73,19 @@
     )(meta)
 
 
-def pack_first(embeds, twin, dest, twin_dest, lengths, gain, start, rows, depth, groups_y):
-    tiles, tile_rows, width = embeds.shape
+def pack_first(sources, lengths, gain, start, rows, depth, groups_y):
+    tiles, tile_rows, width = sources[0][0].shape
+    count = len(sources)
     order = shift_order(depth)
     pairs = depth // 2
-
-    def kernel(dest_ref, twin_dest_ref, len_ref, x_ref, twin_ref, gain_ref, *rest):
-        outs = rest[:pairs]
-        xin, y, source, sem_in, sem_out = rest[pairs:]
+    slot_shape = (rows, width) if count == 1 else (count, rows, width)
+
+    def kernel(*refs):
+        dests = refs[:count]
+        inputs = refs[count : 2 * count]
+        len_ref, gain_ref = refs[2 * count : 2 * count + 2]
+        outs = refs[2 * count + 2 : 2 * count + 2 + pairs]
+        xin, y, source, sem_in, sem_out = refs[2 * count + 2 + pairs :]
         gz = lax.axis_index("gz")
         core = lax.rem(gz, 2)
         chip = gz // 2
@@ -92,34 +96,32 @@
 
         each(depth, clear)
 
-        def copy_in(refs, t, slot):
+        def copy_in(n, t, slot):
             return pltpu.make_async_copy(
-                refs.at[t, pl.ds(start, rows)], xin.at[slot], sem_in.at[slot]
+                inputs[n].at[t, pl.ds(start, rows)], xin.at[slot], sem_in.at[slot]
             )
 
-        def note(dests, refs, from_core):
-            def one(t):
-                peer = lax.rem(dests[t], depth)
+        for n in range(count):
+            from_core = core if sources[n][2] == 0 else 1 - core
+
+            def note(t, n=n, from_core=from_core):
+                peer = lax.rem(dests[n][t], depth)
 
                 @pl.when(lax.rem(peer, 2) == core)
                 def _():
                     slot = lax.rem(peer // 2 - chip + pairs, pairs) * 2 + from_core
                     source[slot] = t
-                    copy_in(refs, t, slot).start()
-
-            each(tiles, one)
-
-        note(dest_ref, x_ref, core)
-        note(twin_dest_ref, twin_ref, 1 - core)
+                    copy_in(n, t, slot).start()
+
+            each(tiles, note)
 
         def compute(slot):
             t = source[slot]
 
             @pl.when(t >= 0)
             def _():
-                copy_in(x_ref, t, slot).wait()
-                from_core = lax.rem(slot, 2)
-                tile = (group * depth + chip * 2 + from_core) * tiles + t
+                copy_in(0, t, slot).wait()
+                tile = (group * depth + chip * 2 + lax.rem(slot, 2)) * tiles + t
                 limit = len_ref[tile // TILES_SEQ]
                 values = xin[slot].astype(jnp.float32)
                 meansq = jnp.sum(values * values, axis=-1, keepdims=True) * (1.0 / width)
@@ -130,58 +132,69 @@
 
         each(depth, compute)
 
-        def copy_out(s, from_core):
-            slot = order[s] * 2 + from_core
-            return pltpu.make_async_copy(y.at[slot], outs[s].at[from_core], sem_out.at[slot])
-
-        where = [(s, from_core) for s in range(pairs) for from_core in range(2)]
-        for s, from_core in where:
-            valid = source[order[s] * 2 + from_core] >= 0
-            pl.when(valid)(lambda s=s, from_core=from_core: copy_out(s, from_core).start())
-        for s, from_core in where:
-            valid = source[order[s] * 2 + from_core] >= 0
-            pl.when(valid)(lambda s=s, from_core=from_core: copy_out(s, from_core).wait())
-
-    return pl.pallas_call(
-        kernel,
-        in_specs=[SMEM, SMEM, SMEM, ANY, ANY, VMEM],
+        def copy_out(s, n):
+            if count == 1:
+                slot = order[s] * 2 + (core if sources[0][2] == 0 else 1 - core)
+                return slot, lambda: pltpu.make_async_copy(y.at[slot], outs[s], sem_out.at[slot])
+            slot = order[s] * 2 + n
+            return slot, lambda: pltpu.make_async_copy(y.at[slot], outs[s].at[n], sem_out.at[slot])
+
+        where = [(s, n) for s in range(pairs) for n in range(count)]
+        for s, n in where:
+            slot, copy = copy_out(s, n)
+            pl.when(source[slot] >= 0)(lambda copy=copy: copy().start())
+        for s, n in where:
+            slot, copy = copy_out(s, n)
+            pl.when(source[slot] >= 0)(lambda copy=copy: copy().wait())
+
+    dtype = sources[0][0].dtype
+    return pl.pallas_call(
+        kernel,
+        in_specs=[SMEM] * count + [ANY] * count + [SMEM, VMEM],
         out_specs=[ANY] * pairs,
-        out_shape=[jax.ShapeDtypeStruct((2, rows, width), embeds.dtype)] * pairs,
+        out_shape=[jax.ShapeDtypeStruct(slot_shape, dtype)] * pairs,
         scratch_shapes=[
-            pltpu.VMEM((depth, rows, width), embeds.dtype),
-            pltpu.VMEM((depth, rows, width), embeds.dtype),
+            pltpu.VMEM((depth, rows, width), dtype),
+            pltpu.VMEM((depth, rows, width), dtype),
             pltpu.SMEM((depth,), jnp.int32),
             pltpu.SemaphoreType.DMA((depth,)),
             pltpu.SemaphoreType.DMA((depth,)),
         ],
-    )(dest, twin_dest, lengths, embeds, twin, gain.reshape(1, width))
-
-
-def pack_second(arrived, meta, depth, groups):
-    _, rows, width = arrived[0].shape
-    resident = rows <= RESIDENT_ROWS
+    )(*(d for _, d, _ in sources), *(x for x, _, _ in sources), lengths, gain.reshape(1, width))
+
+
+def pack_second(arrived, meta, depth, groups, resident):
+    rows, width = arrived[0].shape[-2:]
     order = shift_order(depth)
     pairs = depth // 2
+    count = len(arrived)
 
     def kernel(meta_ref, *rest):
-        ins = rest[:pairs]
+        ins = rest[:count]
         if resident:
-            out_ref, sem_out = rest[pairs:]
+            out_ref, sem_out = rest[count:]
         else:
-            out_ref, held, sem_in, sem_out = rest[pairs:]
-        chip = lax.axis_index("gz") // 2
+            out_ref, held, sem_in, sem_out = rest[count:]
+        gz = lax.axis_index("gz")
+        chip = gz // 2
+        core = lax.rem(gz, 2)
+        if count == pairs:
+            pieces = [ins[n // 2].at[n % 2] for n in range(depth)]
+        else:
+            pieces = [ins[n // 2 + pairs * (n % 2)] for n in range(depth)]
 
         dests = []
         for s in range(pairs):
             for from_core in range(2):
-                peer = lax.rem(chip - order[s] + pairs, pairs) * 2 + from_core
+                sender = from_core if count == pairs else lax.rem(core + from_core, 2)
+                peer = lax.rem(chip - order[s] + pairs, pairs) * 2 + sender
                 dests.append(meta_ref[peer, 0, 0])
 
         def inward(n):
-            return pltpu.make_async_copy(ins[n // 2].at[n % 2], held.at[n], sem_in.at[n])
+            return pltpu.make_async_copy(pieces[n], held.at[n], sem_in.at[n])
 
         def outward(n):
-            here = ins[n // 2].at[n % 2] if resident else held.at[n]
+            here = pieces[n] if resident else held.at[n]
             return pltpu.make_async_copy(here, out_ref.at[dests[n] // depth], sem_out.at[n])
 
         if not resident:
@@ -206,25 +219,25 @@
         ]
     return pl.pallas_call(
         kernel,
-        in_specs=[SMEM] + [VMEM if resident else ANY] * pairs,
+        in_specs=[SMEM] + [VMEM if resident else ANY] * count,
         out_specs=ANY,
         out_shape=jax.ShapeDtypeStruct((groups, rows, width), arrived[0].dtype),
         scratch_shapes=scratch + [pltpu.SemaphoreType.DMA((depth,))],
     )(meta, *arrived)
 
 
-def unpack(arrived, meta, packed, start, tile_rows, cap):
+def unpack(arrived, meta, packed, start, tile_rows, cap, resident=False):
     groups, rows, width = arrived.shape
     first = packed is None
-    resident = rows <= RESIDENT_ROWS and not first
-
-    def kernel(meta_ref, in_ref, *rest):
+
+    def kernel(*refs):
+        meta_ref, in_ref, *rest = refs if first else refs[1:]
         if first:
             out_ref, held, sem_in, sem_out, zeros, sem_zero = rest
         elif resident:
-            _, out_ref, sem_out = rest
+            out_ref, sem_out = rest
         else:
-            _, out_ref, held, sem_in, sem_out = rest
+            out_ref, held, sem_in, sem_out = rest
         keys = [meta_ref[g, 0, 0] for g in range(groups)]
 
         def inward(g):
@@ -283,12 +296,12 @@
         ]
     return pl.pallas_call(
         kernel,
-        in_specs=[SMEM, VMEM if resident else ANY] + ([] if first else [ANY]),
+        in_specs=([] if first else [ANY]) + [SMEM, VMEM if resident else ANY],
         out_specs=ANY,
         out_shape=jax.ShapeDtypeStruct((cap, tile_rows, width), arrived.dtype),
         scratch_shapes=scratch,
-        input_output_aliases={} if first else {2: 0},
-    )(meta, arrived, *(() if first else (packed,)))
+        input_output_aliases={} if first else {0: 0},
+    )(*(() if first else (packed,)), meta, arrived)
 
 
 def shards(embeds, dest_device, shuffle_key, lengths, gain):
@@ -310,28 +323,33 @@
     )
     meta, last_meta = lax.optimization_barrier((meta, last_meta))
 
-    crossing = []
-    for start, rows in zip(starts, chunks):
-        sent = pack_first(
-            embeds, twin, dest_device, twin_dest, lengths, gain, start, rows, depth, groups_y
-        )
-        crossing.append(
-            [
-                lax.ppermute(slots, "gz", shift_pairs(depth, shift)) if shift else slots
-                for slots, shift in zip(sent, shift_order(depth))
-            ]
-        )
+    own, other = (embeds, dest_device, 0), (twin, twin_dest, 1)
+    units = [((own,), 0), ((other,), 0)] + [((own, other), c) for c in range(1, len(chunks))]
+    crossing = [[] for _ in chunks]
+    for sources, c in units:
+        sent = pack_first(sources, lengths, gain, starts[c], chunks[c], depth, groups_y)
+        crossing[c] += [
+            lax.ppermute(slots, "gz", shift_pairs(depth, shift)) if shift else slots
+            for slots, shift in zip(sent, shift_order(depth))
+        ]
 
     packed = landed = None
     for c, (start, rows) in enumerate(zip(starts, chunks)):
-        sent = pack_second(crossing[c], meta, depth, groups)
+        resident = c > 0 and c == len(chunks) - 1
+        if resident:
+            crossing[c] = [
+                pltpu.with_memory_space_constraint(slots, pltpu.VMEM) for slots in crossing[c]
+            ]
+        sent = pack_second(crossing[c], meta, depth, groups, resident)
         if c > 0:
             sent, landed = lax.optimization_barrier((sent, landed))
             packed = unpack(
                 landed, last_meta, packed, starts[c - 1], tile_rows, 2 * tiles
             )
         landed = lax.all_to_all(sent, ("gx", "gy"), split_axis=0, concat_axis=0, tiled=True)
-    return unpack(landed, last_meta, packed, starts[-1], tile_rows, 2 * tiles)
+    if resident:
+        landed = pltpu.with_memory_space_constraint(landed, pltpu.VMEM)
+    return unpack(landed, last_meta, packed, starts[-1], tile_rows, 2 * tiles, resident)
 
 
 def solution(mesh):

time: 316 us -> 302 us (0.956)
  waiting for transfers between devices: 126 us -> 99.3 us
  starting transfers between devices: 102 us -> 121 us
  blocking collectives: 34.2 us -> 27.3 us
    ppermute x28 -> x35, starting transfers between devices: 77.3 us -> 96.2 us  [shards(): lax.ppermute(slots, 'gz', shift_pairs(depth, shift))]
    ppermute x28 -> x35, waiting for transfers between devices: 105 us -> 92.9 us  [shards(): lax.ppermute(slots, 'gz', shift_pairs(depth, shift))]
    all_to_all x4, waiting for transfers between devices: 14 us -> 6.44 us  [shards(): lax.all_to_all(sent, ('gx', 'gy'), split_axis=0, concat_axis=0, tiled=True)]
    ppermute x1, waiting for transfers between devices: 6.99 us -> 0.01 us  [shards(): twin_dest = lax.ppermute(dest_device, 'gz', partner)]
    all_to_all x1, blocking collectives: 19.4 us -> 13.4 us  [shards(): meta = lax.all_to_all(meta, 'gz', split_axis=0, concat_axis=0, tiled=True)]
    pallas_call x12 -> x13, Pallas kernels: 42.2 us -> 44.3 us  [the longest x5 20.7 us: pack_first(): pl.pallas_call(kernel, in_specs=[SMEM] * count + [ANY] * count + [SMEM, V...]
  transfers between devices with their start and end apart: 34 -> 41, of which waited for: 23 -> 20; matrix products, arithmetic and copies ran while one was open for 0% -> 0% of each run, Pallas kernels for 11% -> 14%
where the time goes in v2:
time: 302 us; the launch traced here: 299 us
  starting transfers between devices  121 us (40%)
  waiting for transfers between devices  99.3 us (33%)
  Pallas kernels  47.5 us (16%)
  blocking collectives  27.3 us (9%)
  local copies, waits for them, and re-layouts  3.22 us (1%)
    ppermute x35, starting transfers between devices, shards(): lax.ppermute(slots, 'gz', shift_pairs(depth, shift))  96.2 us
    ppermute x35, waiting for transfers between devices, shards(): lax.ppermute(slots, 'gz', shift_pairs(depth, shift))  92.9 us
    all_to_all x4, starting transfers between devices, shards(): lax.all_to_all(sent, ('gx', 'gy'), split_axis=0, concat_axis=0, tiled=True)  24.9 us
    pallas_call x5, Pallas kernels, pack_first(): pl.pallas_call(kernel, in_specs=[SMEM] * count + [ANY] * count + [SMEM, V...  20.7 us
    all_to_all x1, blocking collectives, shards(): lax.all_to_all(last_meta, ('gx', 'gy'), split_axis=0, concat_axis=0, tile...  13.8 us
    all_to_all x1, blocking collectives, shards(): meta = lax.all_to_all(meta, 'gz', split_axis=0, concat_axis=0, tiled=True)  13.4 us
    pallas_call x4, Pallas kernels, unpack(): pl.pallas_call(kernel, in_specs=([] if first else [ANY]) + [SMEM, VMEM if...  12.4 us
    pallas_call x4, Pallas kernels, pack_second(): pl.pallas_call(kernel, in_specs=[SMEM] + [VMEM if resident else ANY] * co...  11.1 us
  transfers between devices with their start and end apart: 41, of which 20 were waited for; matrix products, arithmetic and copies ran while one was open for 0% of the time, Pallas kernels for 14%

profile of v2, /device:TPU:32, one launch (start us, length us, event | category | flops | bytes accessed | tf_op | source)
XLA Modules:
  0.0 299.1 jit_solution(5990835593442276182)
XLA Ops:
  0.0 3.8 %shard_map.59 = (bf16[56,2048]{1,0:T(8,128)(2,1)}, bf16[56,2048]{1,0:T(8,128)(2,1)}, bf16[56,2048]{1,0:T(8,128)(2,1)}, bf16[56,2048]{1,0:T(8,128)(2,1)}, bf16[56...) custom-call(s32[8]{0:T(128)} %refs_0_.7, ...), custom_call_target="tpu_custom_call" | custom-call | tf_op jit(solution)/shard_map/pallas_call | solution.py:151
  3.9 6.6 %collective-permute-start.9 = (bf16[56,2048]{1,0:T(8,128)(2,1)}, bf16[56,2048]{1,0:T(8,128)(2,1)S(1)}, u32[]{:S(2)}, u32[]{:S(2)}) collective-permute-start(bf16[56,2048]{1,0:T(8,128)(2,1)} %get-tuple-element.63), channel_id=1, source_target_pairs={{0,8},{1,9},{2,10},{3,11},{4,12},{5,13},{6,14},{7,15},{8,0},{9,1},... | collective-permute-start | bytes 688136 | tf_op jit(solution)/shard_map/ppermute | solution.py:332
  10.8 4.7 %collective-permute-start.11 = (bf16[56,2048]{1,0:T(8,128)(2,1)}, bf16[56,2048]{1,0:T(8,128)(2,1)S(1)}, u32[]{:S(2)}, u32[]{:S(2)}) collective-permute-start(bf16[56,2048]{1,0:T(8,128)(2,1)} %get-tuple-element.65), channel_id=1, source_target_pairs={{0,10},{1,11},{2,12},{3,13},{4,14},{5,15},{6,0},{7,1},{8,2},{9,3},... | collective-permute-start | bytes 688136 | tf_op jit(solution)/shard_map/ppermute | solution.py:332
  16.0 3.6 %collective-permute-start.13 = (bf16[56,2048]{1,0:T(8,128)(2,1)}, bf16[56,2048]{1,0:T(8,128)(2,1)S(1)}, u32[]{:S(2)}, u32[]{:S(2)}) collective-permute-start(bf16[56,2048]{1,0:T(8,128)(2,1)} %get-tuple-element.67), channel_id=1, source_target_pairs={{0,12},{1,13},{2,14},{3,15},{4,0},{5,1},{6,2},{7,3},{8,4},{9,5},{1... | collective-permute-start | bytes 688136 | tf_op jit(solution)/shard_map/ppermute | solution.py:332
  19.6 3.9 %shard_map.60 = (bf16[56,2048]{1,0:T(8,128)(2,1)}, bf16[56,2048]{1,0:T(8,128)(2,1)}, bf16[56,2048]{1,0:T(8,128)(2,1)}, bf16[56,2048]{1,0:T(8,128)(2,1)}, bf16[56...) custom-call(s32[8]{0:T(128)} %copy-done.31, ...), custom_call_target="tpu_custom_call" | custom-call | tf_op jit(solution)/shard_map/pallas_call | solution.py:151
  24.2 2.9 collective-permute-start.14
  27.1 8.3 %collective-permute-done.10.rest_1_ = bf16[56,2048]{1,0:T(8,128)(2,1)S(1)} collective-permute-done((bf16[56,2048]{1,0:T(8,128)(2,1)}, bf16[56,2048]{1,0:T(8,128)(2,1)S(1)}, u32[]{:S(2)}, u32[]{:S(2)}) %collective-permute-start.10) | collective-permute-done | bytes 229408 | tf_op jit(solution)/shard_map/ppermute | solution.py:332
  35.4 6.3 %collective-permute-start.15 = (bf16[56,2048]{1,0:T(8,128)(2,1)S(1)}, bf16[56,2048]{1,0:T(8,128)(2,1)S(1)}, u32[]{:S(2)}, u32[]{:S(2)}) collective-permute-start(bf16[56,2048]{1,0:T(8,128)(2,1)S(1)} %copy-done.32), channel_id=1, source_target_pairs={{0,14},{1,15},{2,0},{3,1},{4,2},{5,3},{6,4},{7,5},{8,6},{9,7},{10,... | collective-permute-start | bytes 688136 | tf_op jit(solution)/shard_map/ppermute | solution.py:332
  42.7 3.7 %collective-permute-done.12.rest_3_ = bf16[56,2048]{1,0:T(8,128)(2,1)S(1)} collective-permute-done((bf16[56,2048]{1,0:T(8,128)(2,1)}, bf16[56,2048]{1,0:T(8,128)(2,1)S(1)}, u32[]{:S(2)}, u32[]{:S(2)}) %collective-permute-start.12) | collective-permute-done | bytes 229408 | tf_op jit(solution)/shard_map/ppermute | solution.py:332
  46.4 4.9 %collective-permute-start.17 = (bf16[56,2048]{1,0:T(8,128)(2,1)}, bf16[56,2048]{1,0:T(8,128)(2,1)S(1)}, u32[]{:S(2)}, u32[]{:S(2)}) collective-permute-start(bf16[56,2048]{1,0:T(8,128)(2,1)} %get-tuple-element.72), channel_id=1, source_target_pairs={{0,6},{1,7},{2,8},{3,9},{4,10},{5,11},{6,12},{7,13},{8,14},{9,15},... | collective-permute-start | bytes 688136 | tf_op jit(solution)/shard_map/ppermute | solution.py:332
  52.0 2.5 collective-permute-start.19
  56.2 10.3 %collective-permute-done.16.rest_8_ = bf16[56,2048]{1,0:T(8,128)(2,1)S(1)} collective-permute-done((bf16[56,2048]{1,0:T(8,128)(2,1)}, bf16[56,2048]{1,0:T(8,128)(2,1)S(1)}, u32[]{:S(2)}, u32[]{:S(2)}) %collective-permute-start.16) | collective-permute-done | bytes 229408 | tf_op jit(solution)/shard_map/ppermute | solution.py:332
  68.7 6.2 %collective-permute-done.17.rest_9_ = bf16[56,2048]{1,0:T(8,128)(2,1)S(1)} collective-permute-done((bf16[56,2048]{1,0:T(8,128)(2,1)}, bf16[56,2048]{1,0:T(8,128)(2,1)S(1)}, u32[]{:S(2)}, u32[]{:S(2)}) %collective-permute-start.17) | collective-permute-done | bytes 229408 | tf_op jit(solution)/shard_map/ppermute | solution.py:332
  74.9 6.1 %collective-permute-start.22 = (bf16[56,2048]{1,0:T(8,128)(2,1)}, bf16[56,2048]{1,0:T(8,128)(2,1)S(1)}, u32[]{:S(2)}, u32[]{:S(2)}) collective-permute-start(bf16[56,2048]{1,0:T(8,128)(2,1)} %get-tuple-element.77), channel_id=1, source_target_pairs={{0,14},{1,15},{2,0},{3,1},{4,2},{5,3},{6,4},{7,5},{8,6},{9,7},{10,... | collective-permute-start | bytes 688136 | tf_op jit(solution)/shard_map/ppermute | solution.py:332
  82.5 13.4 %all_to_all.30.meta_ref = s32[16,1,128]{2,1,0:T(1,128)} all-to-all(s32[16,1,128]{2,1,0:T(1,128)} %shard_map.55), channel_id=1, replica_groups=mesh['gx'=4,'gy'=4,'gz'=16] {'gz'}, dimensions={0} | all-to-all | bytes 16384 | tf_op jit(solution)/shard_map/all_to_all | solution.py:319
  97.8 13.8 %all_to_all.31.refs_0_.refs_1_ = s32[16,1,128]{2,1,0:T(1,128)} all-to-all(s32[16,1,128]{2,1,0:T(1,128)} %shard_map.56), channel_id=1, replica_groups=mesh['gx'=4,'gy'=4,'gz'=16] {'gx','gy'}, dimensions={0} | all-to-all | bytes 16384 | tf_op jit(solution)/shard_map/all_to_all | solution.py:321
  112.7 3.4 %shard_map.61 = bf16[16,56,2048]{2,1,0:T(8,128)(2,1)} custom-call(s32[16,1,128]{2,1,0:T(1,128)} %all_to_all.30.meta_ref, bf16[56,2048]{1,0:T(8,128)(2,1)} %copy-done.9, bf16[56,2048]{1,0:T(8,128)(2,1)} %copy-done.10, bf16[56,2048]{1,0:T(8,128)(2,1)} %copy-done.11, bf16[56,2048]{1,0:T(8,128)(2,1)} %copy-done.12, bf16[56,2048]{1,0:T(8,128)(2,1)} %copy-done.13, ...), custom_call_target="tpu_custom_call" | custom-call | tf_op jit(solution)/shard_map/pallas_call | solution.py:220
  116.0 4.5 %all-to-all-start.2 = ((bf16[16,56,2048]{2,1,0:T(8,128)(2,1)}), bf16[16,56,2048]{2,1,0:T(8,128)(2,1)}, u32[]{:S(2)}, u32[]{:S(2)}) async-start(bf16[16,56,2048]{2,1,0:T(8,128)(2,1)} %shard_map.61), calls=%async_computation.2 | async-start | bytes 7340032 | tf_op jit(solution)/shard_map/all_to_all | solution.py:349
  120.6 4.6 %shard_map.57 = (bf16[2,32,2048]{2,1,0:T(8,128)(2,1)}, bf16[2,32,2048]{2,1,0:T(8,128)(2,1)}, bf16[2,32,2048]{2,1,0:T(8,128)(2,1)}, bf16[2,32,2048]{2,1,0:T(8,128...) custom-call(s32[8]{0:T(128)} %refs_0_.7, ...), custom_call_target="tpu_custom_call" | custom-call | tf_op jit(solution)/shard_map/pallas_call | solution.py:151
  126.5 4.7 %collective-permute-start.3 = (bf16[2,32,2048]{2,1,0:T(8,128)(2,1)}, bf16[2,32,2048]{2,1,0:T(8,128)(2,1)S(1)}, u32[]{:S(2)}, u32[]{:S(2)}) collective-permute-start(bf16[2,32,2048]{2,1,0:T(8,128)(2,1)} %get-tuple-element.56), channel_id=1, source_target_pairs={{0,6},{1,7},{2,8},{3,9},{4,10},{5,11},{6,12},{7,13},{8,14},{9,15},... | collective-permute-start | bytes 786440 | tf_op jit(solution)/shard_map/ppermute | solution.py:332
  132.8 2.9 collective-permute-start.6
  135.7 10.5 %collective-permute-done.2.rest_0_ = bf16[2,32,2048]{2,1,0:T(8,128)(2,1)S(1)} collective-permute-done((bf16[2,32,2048]{2,1,0:T(8,128)(2,1)}, bf16[2,32,2048]{2,1,0:T(8,128)(2,1)S(1)}, u32[]{:S(2)}, u32[]{:S(2)}) %collective-permute-start.2) | collective-permute-done | bytes 262176 | tf_op jit(solution)/shard_map/ppermute | solution.py:332
  146.2 11.6 %collective-permute-done.3.rest_1_ = bf16[2,32,2048]{2,1,0:T(8,128)(2,1)S(1)} collective-permute-done((bf16[2,32,2048]{2,1,0:T(8,128)(2,1)}, bf16[2,32,2048]{2,1,0:T(8,128)(2,1)S(1)}, u32[]{:S(2)}, u32[]{:S(2)}) %collective-permute-start.3) | collective-permute-done | bytes 262176 | tf_op jit(solution)/shard_map/ppermute | solution.py:332
  158.9 8.9 %collective-permute-done.5.rest_3_ = bf16[2,32,2048]{2,1,0:T(8,128)(2,1)S(1)} collective-permute-done((bf16[2,32,2048]{2,1,0:T(8,128)(2,1)}, bf16[2,32,2048]{2,1,0:T(8,128)(2,1)S(1)}, u32[]{:S(2)}, u32[]{:S(2)}) %collective-permute-start.5) | collective-permute-done | bytes 262176 | tf_op jit(solution)/shard_map/ppermute | solution.py:332
  167.8 3.6 %collective-permute-done.7.rest_5_ = bf16[2,32,2048]{2,1,0:T(8,128)(2,1)S(1)} collective-permute-done((bf16[2,32,2048]{2,1,0:T(8,128)(2,1)}, bf16[2,32,2048]{2,1,0:T(8,128)(2,1)S(1)}, u32[]{:S(2)}, u32[]{:S(2)}) %collective-permute-start.7) | collective-permute-done | bytes 262176 | tf_op jit(solution)/shard_map/ppermute | solution.py:332
  174.1 3.0 %shard_map.58 = bf16[16,32,2048]{2,1,0:T(8,128)(2,1)} custom-call(s32[16,1,128]{2,1,0:T(1,128)} %all_to_all.30.meta_ref, bf16[2,32,2048]{2,1,0:T(8,128)(2,1)} %copy-done.2, bf16[2,32,2048]{2,1,0:T(8,128)(2,1)} %copy-done.3, bf16[2,32,2048]{2,1,0:T(8,128)(2,1)} %copy-done.4, bf16[2,32,2048]{2,1,0:T(8,128)(2,1)} %copy-done.5, bf16[2,32,2048]{2,1,0:T(8,128)(2,1)} %copy-done.6, ...), custom_call_target="tpu_custom_call" | custom-call | tf_op jit(solution)/shard_map/pallas_call | solution.py:220
  177.1 6.6 %all-to-all-start.3 = ((bf16[16,32,2048]{2,1,0:T(8,128)(2,1)}), bf16[16,32,2048]{2,1,0:T(8,128)(2,1)S(1)}, u32[]{:S(2)}, u32[]{:S(2)}) async-start(bf16[16,32,2048]{2,1,0:T(8,128)(2,1)} %shard_map.58), calls=%async_computation.3 | async-start | bytes 4194304 | tf_op jit(solution)/shard_map/all_to_all | solution.py:349
  183.8 4.3 %shard_map.63 = (bf16[2,24,2048]{2,1,0:T(8,128)(2,1)}, bf16[2,24,2048]{2,1,0:T(8,128)(2,1)}, bf16[2,24,2048]{2,1,0:T(8,128)(2,1)}, bf16[2,24,2048]{2,1,0:T(8,128...) custom-call(s32[8]{0:T(128)} %refs_0_.7, ...), custom_call_target="tpu_custom_call" | custom-call | tf_op jit(solution)/shard_map/pallas_call | solution.py:151
  188.1 3.4 %collective-permute-start.23 = (bf16[2,24,2048]{2,1,0:T(8,128)(2,1)}, bf16[2,24,2048]{2,1,0:T(8,128)(2,1)S(1)}, u32[]{:S(2)}, u32[]{:S(2)}) collective-permute-start(bf16[2,24,2048]{2,1,0:T(8,128)(2,1)} %get-tuple-element.80), channel_id=1, source_target_pairs={{0,8},{1,9},{2,10},{3,11},{4,12},{5,13},{6,14},{7,15},{8,0},{9,1},... | collective-permute-start | bytes 589832 | tf_op jit(solution)/shard_map/ppermute | solution.py:332
  191.5 3.0 %collective-permute-start.24 = (bf16[2,24,2048]{2,1,0:T(8,128)(2,1)}, bf16[2,24,2048]{2,1,0:T(8,128)(2,1)S(1)}, u32[]{:S(2)}, u32[]{:S(2)}) collective-permute-start(bf16[2,24,2048]{2,1,0:T(8,128)(2,1)} %get-tuple-element.81), channel_id=1, source_target_pairs={{0,6},{1,7},{2,8},{3,9},{4,10},{5,11},{6,12},{7,13},{8,14},{9,15},... | collective-permute-start | bytes 589832 | tf_op jit(solution)/shard_map/ppermute | solution.py:332
  196.5 4.1 %collective-permute-start.27 = (bf16[2,24,2048]{2,1,0:T(8,128)(2,1)}, bf16[2,24,2048]{2,1,0:T(8,128)(2,1)S(1)}, u32[]{:S(2)}, u32[]{:S(2)}) collective-permute-start(bf16[2,24,2048]{2,1,0:T(8,128)(2,1)} %get-tuple-element.84), channel_id=1, source_target_pairs={{0,12},{1,13},{2,14},{3,15},{4,0},{5,1},{6,2},{7,3},{8,4},{9,5},{1... | collective-permute-start | bytes 589832 | tf_op jit(solution)/shard_map/ppermute | solution.py:332
  201.8 5.4 %collective-permute-start.28 = (bf16[2,24,2048]{2,1,0:T(8,128)(2,1)}, bf16[2,24,2048]{2,1,0:T(8,128)(2,1)S(1)}, u32[]{:S(2)}, u32[]{:S(2)}) collective-permute-start(bf16[2,24,2048]{2,1,0:T(8,128)(2,1)} %get-tuple-element.85), channel_id=1, source_target_pairs={{0,2},{1,3},{2,4},{3,5},{4,6},{5,7},{6,8},{7,9},{8,10},{9,11},{10,... | collective-permute-start | bytes 589832 | tf_op jit(solution)/shard_map/ppermute | solution.py:332
  207.2 9.8 %collective-permute-done.24.rest_1_ = bf16[2,24,2048]{2,1,0:T(8,128)(2,1)S(1)} collective-permute-done((bf16[2,24,2048]{2,1,0:T(8,128)(2,1)}, bf16[2,24,2048]{2,1,0:T(8,128)(2,1)S(1)}, u32[]{:S(2)}, u32[]{:S(2)}) %collective-permute-start.24) | collective-permute-done | bytes 196640 | tf_op jit(solution)/shard_map/ppermute | solution.py:332
  217.0 4.1 %collective-permute-start.29 = (bf16[2,24,2048]{2,1,0:T(8,128)(2,1)}, bf16[2,24,2048]{2,1,0:T(8,128)(2,1)S(1)}, u32[]{:S(2)}, u32[]{:S(2)}) collective-permute-start(bf16[2,24,2048]{2,1,0:T(8,128)(2,1)} %get-tuple-element.86), channel_id=1, source_target_pairs={{0,14},{1,15},{2,0},{3,1},{4,2},{5,3},{6,4},{7,5},{8,6},{9,7},{10,... | collective-permute-start | bytes 589832 | tf_op jit(solution)/shard_map/ppermute | solution.py:332
  221.1 3.1 %collective-permute-done.26.rest_3_ = bf16[2,24,2048]{2,1,0:T(8,128)(2,1)S(1)} collective-permute-done((bf16[2,24,2048]{2,1,0:T(8,128)(2,1)}, bf16[2,24,2048]{2,1,0:T(8,128)(2,1)S(1)}, u32[]{:S(2)}, u32[]{:S(2)}) %collective-permute-start.26) | collective-permute-done | bytes 196640 | tf_op jit(solution)/shard_map/ppermute | solution.py:332
  227.5 3.0 shard_map.64
  230.5 6.7 %all-to-all-start.4 = ((bf16[16,24,2048]{2,1,0:T(8,128)(2,1)}), bf16[16,24,2048]{2,1,0:T(8,128)(2,1)}, u32[]{:S(2)}, u32[]{:S(2)}) async-start(bf16[16,24,2048]{2,1,0:T(8,128)(2,1)} %shard_map.64), calls=%async_computation.4 | async-start | bytes 3145728 | tf_op jit(solution)/shard_map/all_to_all | solution.py:349
  237.1 4.1 %shard_map.66 = (bf16[2,16,2048]{2,1,0:T(8,128)(2,1)}, bf16[2,16,2048]{2,1,0:T(8,128)(2,1)}, bf16[2,16,2048]{2,1,0:T(8,128)(2,1)}, bf16[2,16,2048]{2,1,0:T(8,128...) custom-call(s32[8]{0:T(128)} %refs_0_.7, ...), custom_call_target="tpu_custom_call" | custom-call | tf_op jit(solution)/shard_map/pallas_call | solution.py:151
  241.3 4.4 %collective-permute-start.30 = (bf16[2,16,2048]{2,1,0:T(8,128)(2,1)}, bf16[2,16,2048]{2,1,0:T(8,128)(2,1)S(1)}, u32[]{:S(2)}, u32[]{:S(2)}) collective-permute-start(bf16[2,16,2048]{2,1,0:T(8,128)(2,1)} %get-tuple-element.90), channel_id=1, source_target_pairs={{0,8},{1,9},{2,10},{3,11},{4,12},{5,13},{6,14},{7,15},{8,0},{9,1},... | collective-permute-start | bytes 393224 | tf_op jit(solution)/shard_map/ppermute | solution.py:332
  245.6 2.9 collective-permute-start.31
  250.7 4.1 %collective-permute-start.34 = (bf16[2,16,2048]{2,1,0:T(8,128)(2,1)}, bf16[2,16,2048]{2,1,0:T(8,128)(2,1)S(1)}, u32[]{:S(2)}, u32[]{:S(2)}) collective-permute-start(bf16[2,16,2048]{2,1,0:T(8,128)(2,1)} %get-tuple-element.94), channel_id=1, source_target_pairs={{0,12},{1,13},{2,14},{3,15},{4,0},{5,1},{6,2},{7,3},{8,4},{9,5},{1... | collective-permute-start | bytes 393224 | tf_op jit(solution)/shard_map/ppermute | solution.py:332
  256.1 6.4 %collective-permute-done.31.rest_1_ = bf16[2,16,2048]{2,1,0:T(8,128)(2,1)S(1)} collective-permute-done((bf16[2,16,2048]{2,1,0:T(8,128)(2,1)}, bf16[2,16,2048]{2,1,0:T(8,128)(2,1)S(1)}, u32[]{:S(2)}, u32[]{:S(2)}) %collective-permute-start.31) | collective-permute-done | bytes 131104 | tf_op jit(solution)/shard_map/ppermute | solution.py:332
  262.4 4.3 %collective-permute-start.36 = (bf16[2,16,2048]{2,1,0:T(8,128)(2,1)}, bf16[2,16,2048]{2,1,0:T(8,128)(2,1)S(1)}, u32[]{:S(2)}, u32[]{:S(2)}) collective-permute-start(bf16[2,16,2048]{2,1,0:T(8,128)(2,1)} %get-tuple-element.96), channel_id=1, source_target_pairs={{0,14},{1,15},{2,0},{3,1},{4,2},{5,3},{6,4},{7,5},{8,6},{9,7},{10,... | collective-permute-start | bytes 393224 | tf_op jit(solution)/shard_map/ppermute | solution.py:332
  273.0 7.1 %all-to-all-start.5 = ((bf16[16,16,2048]{2,1,0:T(8,128)(2,1)}), bf16[16,16,2048]{2,1,0:T(8,128)(2,1)S(1)}, u32[]{:S(2)}, u32[]{:S(2)}) async-start(bf16[16,16,2048]{2,1,0:T(8,128)(2,1)} %shard_map.67), calls=%async_computation.5 | async-start | bytes 2097152 | tf_op jit(solution)/shard_map/all_to_all | solution.py:349
  280.0 4.3 %shard_map.62.refs_0_ = bf16[16,128,2048]{2,1,0:T(8,128)(2,1)} custom-call(s32[16,1,128]{2,1,0:T(1,128)} %all_to_all.31.refs_0_.refs_1_, bf16[16,56,2048]{2,1,0:T(8,128)(2,1)} %all-to-all-done.2.refs_1_), custom_call_target="tpu_custom_call" | custom-call | tf_op jit(solution)/shard_map/pallas_call | solution.py:297
  284.4 3.1 %shard_map.65.refs_0_ = bf16[16,128,2048]{2,1,0:T(8,128)(2,1)} custom-call(bf16[16,128,2048]{2,1,0:T(8,128)(2,1)} %shard_map.62.refs_0_, s32[16,1,128]{2,1,0:T(1,128)} %all_to_all.31.refs_0_.refs_1_, bf16[16,32,2048]{2,1,0:T(8,128)(2,1)} %copy-done.1), custom_call_target="tpu_custom_call", output_to_operand_aliasing={{}: (0, {})} | custom-call | tf_op jit(solution)/shard_map/pallas_call | solution.py:297
  287.5 3.0 %shard_map.68.refs_0_ = bf16[16,128,2048]{2,1,0:T(8,128)(2,1)} custom-call(bf16[16,128,2048]{2,1,0:T(8,128)(2,1)} %shard_map.65.refs_0_, s32[16,1,128]{2,1,0:T(1,128)} %all_to_all.31.refs_0_.refs_1_, bf16[16,24,2048]{2,1,0:T(8,128)(2,1)} %all-to-all-done.4.refs_2_), custom_call_target="tpu_custom_call", output_to_operand_aliasing={{}: (0, {})} | custom-call | tf_op jit(solution)/shard_map/pallas_call | solution.py:297
  290.5 6.4 %all-to-all-done.5.refs_2_ = bf16[16,16,2048]{2,1,0:T(8,128)(2,1)S(1)} async-done(((bf16[16,16,2048]{2,1,0:T(8,128)(2,1)}), bf16[16,16,2048]{2,1,0:T(8,128)(2,1)S(1)}, u32[]{:S(2)}, u32[]{:S(2)}) %all-to-all-start.5) | async-done | bytes 1048608 | tf_op jit(solution)/shard_map/all_to_all | solution.py:349
  (119 shorter events, 36.2 us)
Async XLA Ops:
  0.0 16.0 %collective-permute-start.1 = (bf16[8,128,2048]{2,1,0:T(8,128)(2,1)}, bf16[8,128,2048]{2,1,0:T(8,128)(2,1)}, u32[]{:S(2)}, u32[]{:S(2)}) collective-permute-start(bf16[8,128,2048]{2,1,0:T(8,128)(2,1)} %refs_2_.9), channel_id=1, source_target_pairs={{0,1},{1,0},{2,3},{3,2},{4,5},{5,4},{6,7},{7,6},{8,9},{9,8},{10,11... | collective-permute-start | bytes 12582920 | tf_op jit(solution)/shard_map/ppermute | solution.py:316
  3.9 20.3 %collective-permute-start.9 = (bf16[56,2048]{1,0:T(8,128)(2,1)}, bf16[56,2048]{1,0:T(8,128)(2,1)S(1)}, u32[]{:S(2)}, u32[]{:S(2)}) collective-permute-start(bf16[56,2048]{1,0:T(8,128)(2,1)} %get-tuple-element.63), channel_id=1, source_target_pairs={{0,8},{1,9},{2,10},{3,11},{4,12},{5,13},{6,14},{7,15},{8,0},{9,1},... | collective-permute-start | bytes 688136 | tf_op jit(solution)/shard_map/ppermute | solution.py:332
  10.4 24.9 %collective-permute-start.10 = (bf16[56,2048]{1,0:T(8,128)(2,1)}, bf16[56,2048]{1,0:T(8,128)(2,1)S(1)}, u32[]{:S(2)}, u32[]{:S(2)}) collective-permute-start(bf16[56,2048]{1,0:T(8,128)(2,1)} %get-tuple-element.64), channel_id=1, source_target_pairs={{0,6},{1,7},{2,8},{3,9},{4,10},{5,11},{6,12},{7,13},{8,14},{9,15},... | collective-permute-start | bytes 688136 | tf_op jit(solution)/shard_map/ppermute | solution.py:332
  10.8 4.7 %collective-permute-start = (s32[8]{0:T(128)S(1)}, s32[8]{0:T(128)S(1)}, u32[]{:S(2)}, u32[]{:S(2)}) collective-permute-start(s32[8]{0:T(128)S(1)} %copy-done.30), channel_id=1, source_target_pairs={{0,1},{1,0},{2,3},{3,2},{4,5},{5,4},{6,7},{7,6},{8,9},{9,8},{10,11... | collective-permute-start | bytes 104 | tf_op jit(solution)/shard_map/ppermute | solution.py:317
  10.8 31.0 %collective-permute-start.11 = (bf16[56,2048]{1,0:T(8,128)(2,1)}, bf16[56,2048]{1,0:T(8,128)(2,1)S(1)}, u32[]{:S(2)}, u32[]{:S(2)}) collective-permute-start(bf16[56,2048]{1,0:T(8,128)(2,1)} %get-tuple-element.65), channel_id=1, source_target_pairs={{0,10},{1,11},{2,12},{3,13},{4,14},{5,15},{6,0},{7,1},{8,2},{9,3},... | collective-permute-start | bytes 688136 | tf_op jit(solution)/shard_map/ppermute | solution.py:332
  15.5 30.9 %collective-permute-start.12 = (bf16[56,2048]{1,0:T(8,128)(2,1)}, bf16[56,2048]{1,0:T(8,128)(2,1)S(1)}, u32[]{:S(2)}, u32[]{:S(2)}) collective-permute-start(bf16[56,2048]{1,0:T(8,128)(2,1)} %get-tuple-element.66), channel_id=1, source_target_pairs={{0,4},{1,5},{2,6},{3,7},{4,8},{5,9},{6,10},{7,11},{8,12},{9,13},{1... | collective-permute-start | bytes 688136 | tf_op jit(solution)/shard_map/ppermute | solution.py:332
  16.0 35.3 %collective-permute-start.13 = (bf16[56,2048]{1,0:T(8,128)(2,1)}, bf16[56,2048]{1,0:T(8,128)(2,1)S(1)}, u32[]{:S(2)}, u32[]{:S(2)}) collective-permute-start(bf16[56,2048]{1,0:T(8,128)(2,1)} %get-tuple-element.67), channel_id=1, source_target_pairs={{0,12},{1,13},{2,14},{3,15},{4,0},{5,1},{6,2},{7,3},{8,4},{9,5},{1... | collective-permute-start | bytes 688136 | tf_op jit(solution)/shard_map/ppermute | solution.py:332
  24.2 87.5 %copy-start.9 = (bf16[56,2048]{1,0:T(8,128)(2,1)}, bf16[56,2048]{1,0:T(8,128)(2,1)S(1)}, u32[]{:S(2)}) copy-start(bf16[56,2048]{1,0:T(8,128)(2,1)S(1)} %collective-permute-done.9.rest_0_) | copy-start | bytes 688132
  24.2 27.8 %collective-permute-start.14 = (bf16[56,2048]{1,0:T(8,128)(2,1)S(1)}, bf16[56,2048]{1,0:T(8,128)(2,1)S(1)}, u32[]{:S(2)}, u32[]{:S(2)}) collective-permute-start(bf16[56,2048]{1,0:T(8,128)(2,1)S(1)} %copy-done.33), channel_id=1, source_target_pairs={{0,2},{1,3},{2,4},{3,5},{4,6},{5,7},{6,8},{7,9},{8,10},{9,11},{10,... | collective-permute-start | bytes 688136 | tf_op jit(solution)/shard_map/ppermute | solution.py:332
  35.4 76.3 %copy-start.10 = (bf16[56,2048]{1,0:T(8,128)(2,1)}, bf16[56,2048]{1,0:T(8,128)(2,1)S(1)}, u32[]{:S(2)}) copy-start(bf16[56,2048]{1,0:T(8,128)(2,1)S(1)} %collective-permute-done.10.rest_1_) | copy-start | bytes 688132
  35.4 19.1 %collective-permute-start.15 = (bf16[56,2048]{1,0:T(8,128)(2,1)S(1)}, bf16[56,2048]{1,0:T(8,128)(2,1)S(1)}, u32[]{:S(2)}, u32[]{:S(2)}) collective-permute-start(bf16[56,2048]{1,0:T(8,128)(2,1)S(1)} %copy-done.32), channel_id=1, source_target_pairs={{0,14},{1,15},{2,0},{3,1},{4,2},{5,3},{6,4},{7,5},{8,6},{9,7},{10,... | collective-permute-start | bytes 688136 | tf_op jit(solution)/shard_map/ppermute | solution.py:332
  41.7 70.0 %copy-start.11 = (bf16[56,2048]{1,0:T(8,128)(2,1)}, bf16[56,2048]{1,0:T(8,128)(2,1)S(1)}, u32[]{:S(2)}) copy-start(bf16[56,2048]{1,0:T(8,128)(2,1)S(1)} %collective-permute-done.11.rest_2_) | copy-start | bytes 688132
  41.7 24.7 %collective-permute-start.16 = (bf16[56,2048]{1,0:T(8,128)(2,1)}, bf16[56,2048]{1,0:T(8,128)(2,1)S(1)}, u32[]{:S(2)}, u32[]{:S(2)}) collective-permute-start(bf16[56,2048]{1,0:T(8,128)(2,1)} %get-tuple-element.71), channel_id=1, source_target_pairs={{0,8},{1,9},{2,10},{3,11},{4,12},{5,13},{6,14},{7,15},{8,0},{9,1},... | collective-permute-start | bytes 688136 | tf_op jit(solution)/shard_map/ppermute | solution.py:332
  46.4 65.3 %copy-start.12 = (bf16[56,2048]{1,0:T(8,128)(2,1)}, bf16[56,2048]{1,0:T(8,128)(2,1)S(1)}, u32[]{:S(2)}) copy-start(bf16[56,2048]{1,0:T(8,128)(2,1)S(1)} %collective-permute-done.12.rest_3_) | copy-start | bytes 688132
  46.4 28.5 %collective-permute-start.17 = (bf16[56,2048]{1,0:T(8,128)(2,1)}, bf16[56,2048]{1,0:T(8,128)(2,1)S(1)}, u32[]{:S(2)}, u32[]{:S(2)}) collective-permute-start(bf16[56,2048]{1,0:T(8,128)(2,1)} %get-tuple-element.72), channel_id=1, source_target_pairs={{0,6},{1,7},{2,8},{3,9},{4,10},{5,11},{6,12},{7,13},{8,14},{9,15},... | collective-permute-start | bytes 688136 | tf_op jit(solution)/shard_map/ppermute | solution.py:332
  51.4 60.4 %copy-start.13 = (bf16[56,2048]{1,0:T(8,128)(2,1)}, bf16[56,2048]{1,0:T(8,128)(2,1)S(1)}, u32[]{:S(2)}) copy-start(bf16[56,2048]{1,0:T(8,128)(2,1)S(1)} %collective-permute-done.13.rest_4_) | copy-start | bytes 688132
  51.4 60.2 %collective-permute-start.18 = (bf16[56,2048]{1,0:T(8,128)(2,1)}, bf16[56,2048]{1,0:T(8,128)(2,1)S(1)}, u32[]{:S(2)}, u32[]{:S(2)}) collective-permute-start(bf16[56,2048]{1,0:T(8,128)(2,1)} %get-tuple-element.73), channel_id=1, source_target_pairs={{0,10},{1,11},{2,12},{3,13},{4,14},{5,15},{6,0},{7,1},{8,2},{9,3},... | collective-permute-start | bytes 688136 | tf_op jit(solution)/shard_map/ppermute | solution.py:332
  52.0 59.7 %copy-start.14 = (bf16[56,2048]{1,0:T(8,128)(2,1)}, bf16[56,2048]{1,0:T(8,128)(2,1)S(1)}, u32[]{:S(2)}) copy-start(bf16[56,2048]{1,0:T(8,128)(2,1)S(1)} %collective-permute-done.14.rest_5_) | copy-start | bytes 688132
  52.0 59.6 %collective-permute-start.19 = (bf16[56,2048]{1,0:T(8,128)(2,1)}, bf16[56,2048]{1,0:T(8,128)(2,1)S(1)}, u32[]{:S(2)}, u32[]{:S(2)}) collective-permute-start(bf16[56,2048]{1,0:T(8,128)(2,1)} %get-tuple-element.74), channel_id=1, source_target_pairs={{0,4},{1,5},{2,6},{3,7},{4,8},{5,9},{6,10},{7,11},{8,12},{9,13},{1... | collective-permute-start | bytes 688136 | tf_op jit(solution)/shard_map/ppermute | solution.py:332
  54.5 57.2 %copy-start.15 = (bf16[56,2048]{1,0:T(8,128)(2,1)}, bf16[56,2048]{1,0:T(8,128)(2,1)S(1)}, u32[]{:S(2)}) copy-start(bf16[56,2048]{1,0:T(8,128)(2,1)S(1)} %collective-permute-done.15.rest_6_) | copy-start | bytes 688132
  54.5 57.1 %collective-permute-start.20 = (bf16[56,2048]{1,0:T(8,128)(2,1)}, bf16[56,2048]{1,0:T(8,128)(2,1)S(1)}, u32[]{:S(2)}, u32[]{:S(2)}) collective-permute-start(bf16[56,2048]{1,0:T(8,128)(2,1)} %get-tuple-element.75), channel_id=1, source_target_pairs={{0,12},{1,13},{2,14},{3,15},{4,0},{5,1},{6,2},{7,3},{8,4},{9,5},{1... | collective-permute-start | bytes 688136 | tf_op jit(solution)/shard_map/ppermute | solution.py:332
  66.5 45.2 %collective-permute-start.21 = (bf16[56,2048]{1,0:T(8,128)(2,1)}, bf16[56,2048]{1,0:T(8,128)(2,1)S(1)}, u32[]{:S(2)}, u32[]{:S(2)}) collective-permute-start(bf16[56,2048]{1,0:T(8,128)(2,1)} %get-tuple-element.76), channel_id=1, source_target_pairs={{0,2},{1,3},{2,4},{3,5},{4,6},{5,7},{6,8},{7,9},{8,10},{9,11},{10,... | collective-permute-start | bytes 688136 | tf_op jit(solution)/shard_map/ppermute | solution.py:332
  74.9 36.8 %collective-permute-start.22 = (bf16[56,2048]{1,0:T(8,128)(2,1)}, bf16[56,2048]{1,0:T(8,128)(2,1)S(1)}, u32[]{:S(2)}, u32[]{:S(2)}) collective-permute-start(bf16[56,2048]{1,0:T(8,128)(2,1)} %get-tuple-element.77), channel_id=1, source_target_pairs={{0,14},{1,15},{2,0},{3,1},{4,2},{5,3},{6,4},{7,5},{8,6},{9,7},{10,... | collective-permute-start | bytes 688136 | tf_op jit(solution)/shard_map/ppermute | solution.py:332
  116.0 61.1 %all-to-all-start.2 = ((bf16[16,56,2048]{2,1,0:T(8,128)(2,1)}), bf16[16,56,2048]{2,1,0:T(8,128)(2,1)}, u32[]{:S(2)}, u32[]{:S(2)}) async-start(bf16[16,56,2048]{2,1,0:T(8,128)(2,1)} %shard_map.61), calls=%async_computation.2 | async-start | bytes 7340032 | tf_op jit(solution)/shard_map/all_to_all | solution.py:349
  125.2 21.0 %collective-permute-start.2 = (bf16[2,32,2048]{2,1,0:T(8,128)(2,1)}, bf16[2,32,2048]{2,1,0:T(8,128)(2,1)S(1)}, u32[]{:S(2)}, u32[]{:S(2)}) collective-permute-start(bf16[2,32,2048]{2,1,0:T(8,128)(2,1)} %get-tuple-element.55), channel_id=1, source_target_pairs={{0,8},{1,9},{2,10},{3,11},{4,12},{5,13},{6,14},{7,15},{8,0},{9,1},... | collective-permute-start | bytes 786440 | tf_op jit(solution)/shard_map/ppermute | solution.py:332
  126.5 31.3 %collective-permute-start.3 = (bf16[2,32,2048]{2,1,0:T(8,128)(2,1)}, bf16[2,32,2048]{2,1,0:T(8,128)(2,1)S(1)}, u32[]{:S(2)}, u32[]{:S(2)}) collective-permute-start(bf16[2,32,2048]{2,1,0:T(8,128)(2,1)} %get-tuple-element.56), channel_id=1, source_target_pairs={{0,6},{1,7},{2,8},{3,9},{4,10},{5,11},{6,12},{7,13},{8,14},{9,15},... | collective-permute-start | bytes 786440 | tf_op jit(solution)/shard_map/ppermute | solution.py:332
  131.2 27.7 %collective-permute-start.4 = (bf16[2,32,2048]{2,1,0:T(8,128)(2,1)}, bf16[2,32,2048]{2,1,0:T(8,128)(2,1)S(1)}, u32[]{:S(2)}, u32[]{:S(2)}) collective-permute-start(bf16[2,32,2048]{2,1,0:T(8,128)(2,1)} %get-tuple-element.57), channel_id=1, source_target_pairs={{0,10},{1,11},{2,12},{3,13},{4,14},{5,15},{6,0},{7,1},{8,2},{9,3},... | collective-permute-start | bytes 786440 | tf_op jit(solution)/shard_map/ppermute | solution.py:332
  131.6 36.2 %collective-permute-start.5 = (bf16[2,32,2048]{2,1,0:T(8,128)(2,1)}, bf16[2,32,2048]{2,1,0:T(8,128)(2,1)S(1)}, u32[]{:S(2)}, u32[]{:S(2)}) collective-permute-start(bf16[2,32,2048]{2,1,0:T(8,128)(2,1)} %get-tuple-element.58), channel_id=1, source_target_pairs={{0,4},{1,5},{2,6},{3,7},{4,8},{5,9},{6,10},{7,11},{8,12},{9,13},{1... | collective-permute-start | bytes 786440 | tf_op jit(solution)/shard_map/ppermute | solution.py:332
  132.8 35.0 %collective-permute-start.6 = (bf16[2,32,2048]{2,1,0:T(8,128)(2,1)}, bf16[2,32,2048]{2,1,0:T(8,128)(2,1)S(1)}, u32[]{:S(2)}, u32[]{:S(2)}) collective-permute-start(bf16[2,32,2048]{2,1,0:T(8,128)(2,1)} %get-tuple-element.59), channel_id=1, source_target_pairs={{0,12},{1,13},{2,14},{3,15},{4,0},{5,1},{6,2},{7,3},{8,4},{9,5},{1... | collective-permute-start | bytes 786440 | tf_op jit(solution)/shard_map/ppermute | solution.py:332
  146.2 25.2 %collective-permute-start.7 = (bf16[2,32,2048]{2,1,0:T(8,128)(2,1)}, bf16[2,32,2048]{2,1,0:T(8,128)(2,1)S(1)}, u32[]{:S(2)}, u32[]{:S(2)}) collective-permute-start(bf16[2,32,2048]{2,1,0:T(8,128)(2,1)} %get-tuple-element.60), channel_id=1, source_target_pairs={{0,2},{1,3},{2,4},{3,5},{4,6},{5,7},{6,8},{7,9},{8,10},{9,11},{10,... | collective-permute-start | bytes 786440 | tf_op jit(solution)/shard_map/ppermute | solution.py:332
  157.8 15.5 %collective-permute-start.8 = (bf16[2,32,2048]{2,1,0:T(8,128)(2,1)}, bf16[2,32,2048]{2,1,0:T(8,128)(2,1)S(1)}, u32[]{:S(2)}, u32[]{:S(2)}) collective-permute-start(bf16[2,32,2048]{2,1,0:T(8,128)(2,1)} %get-tuple-element.61), channel_id=1, source_target_pairs={{0,14},{1,15},{2,0},{3,1},{4,2},{5,3},{6,4},{7,5},{8,6},{9,7},{10,... | collective-permute-start | bytes 786440 | tf_op jit(solution)/shard_map/ppermute | solution.py:332
  177.1 53.3 %all-to-all-start.3 = ((bf16[16,32,2048]{2,1,0:T(8,128)(2,1)}), bf16[16,32,2048]{2,1,0:T(8,128)(2,1)S(1)}, u32[]{:S(2)}, u32[]{:S(2)}) async-start(bf16[16,32,2048]{2,1,0:T(8,128)(2,1)} %shard_map.58), calls=%async_computation.3 | async-start | bytes 4194304 | tf_op jit(solution)/shard_map/all_to_all | solution.py:349
  188.1 13.8 %collective-permute-start.23 = (bf16[2,24,2048]{2,1,0:T(8,128)(2,1)}, bf16[2,24,2048]{2,1,0:T(8,128)(2,1)S(1)}, u32[]{:S(2)}, u32[]{:S(2)}) collective-permute-start(bf16[2,24,2048]{2,1,0:T(8,128)(2,1)} %get-tuple-element.80), channel_id=1, source_target_pairs={{0,8},{1,9},{2,10},{3,11},{4,12},{5,13},{6,14},{7,15},{8,0},{9,1},... | collective-permute-start | bytes 589832 | tf_op jit(solution)/shard_map/ppermute | solution.py:332
  191.5 25.6 %collective-permute-start.24 = (bf16[2,24,2048]{2,1,0:T(8,128)(2,1)}, bf16[2,24,2048]{2,1,0:T(8,128)(2,1)S(1)}, u32[]{:S(2)}, u32[]{:S(2)}) collective-permute-start(bf16[2,24,2048]{2,1,0:T(8,128)(2,1)} %get-tuple-element.81), channel_id=1, source_target_pairs={{0,6},{1,7},{2,8},{3,9},{4,10},{5,11},{6,12},{7,13},{8,14},{9,15},... | collective-permute-start | bytes 589832 | tf_op jit(solution)/shard_map/ppermute | solution.py:332
  194.5 26.6 %collective-permute-start.25 = (bf16[2,24,2048]{2,1,0:T(8,128)(2,1)}, bf16[2,24,2048]{2,1,0:T(8,128)(2,1)S(1)}, u32[]{:S(2)}, u32[]{:S(2)}) collective-permute-start(bf16[2,24,2048]{2,1,0:T(8,128)(2,1)} %get-tuple-element.82), channel_id=1, source_target_pairs={{0,10},{1,11},{2,12},{3,13},{4,14},{5,15},{6,0},{7,1},{8,2},{9,3},... | collective-permute-start | bytes 589832 | tf_op jit(solution)/shard_map/ppermute | solution.py:332
  196.5 27.7 %collective-permute-start.26 = (bf16[2,24,2048]{2,1,0:T(8,128)(2,1)}, bf16[2,24,2048]{2,1,0:T(8,128)(2,1)S(1)}, u32[]{:S(2)}, u32[]{:S(2)}) collective-permute-start(bf16[2,24,2048]{2,1,0:T(8,128)(2,1)} %get-tuple-element.83), channel_id=1, source_target_pairs={{0,4},{1,5},{2,6},{3,7},{4,8},{5,9},{6,10},{7,11},{8,12},{9,13},{1... | collective-permute-start | bytes 589832 | tf_op jit(solution)/shard_map/ppermute | solution.py:332
  196.5 27.8 %collective-permute-start.27 = (bf16[2,24,2048]{2,1,0:T(8,128)(2,1)}, bf16[2,24,2048]{2,1,0:T(8,128)(2,1)S(1)}, u32[]{:S(2)}, u32[]{:S(2)}) collective-permute-start(bf16[2,24,2048]{2,1,0:T(8,128)(2,1)} %get-tuple-element.84), channel_id=1, source_target_pairs={{0,12},{1,13},{2,14},{3,15},{4,0},{5,1},{6,2},{7,3},{8,4},{9,5},{1... | collective-permute-start | bytes 589832 | tf_op jit(solution)/shard_map/ppermute | solution.py:332
  201.8 24.4 %collective-permute-start.28 = (bf16[2,24,2048]{2,1,0:T(8,128)(2,1)}, bf16[2,24,2048]{2,1,0:T(8,128)(2,1)S(1)}, u32[]{:S(2)}, u32[]{:S(2)}) collective-permute-start(bf16[2,24,2048]{2,1,0:T(8,128)(2,1)} %get-tuple-element.85), channel_id=1, source_target_pairs={{0,2},{1,3},{2,4},{3,5},{4,6},{5,7},{6,8},{7,9},{8,10},{9,11},{10,... | collective-permute-start | bytes 589832 | tf_op jit(solution)/shard_map/ppermute | solution.py:332
  217.0 9.8 %collective-permute-start.29 = (bf16[2,24,2048]{2,1,0:T(8,128)(2,1)}, bf16[2,24,2048]{2,1,0:T(8,128)(2,1)S(1)}, u32[]{:S(2)}, u32[]{:S(2)}) collective-permute-start(bf16[2,24,2048]{2,1,0:T(8,128)(2,1)} %get-tuple-element.86), channel_id=1, source_target_pairs={{0,14},{1,15},{2,0},{3,1},{4,2},{5,3},{6,4},{7,5},{8,6},{9,7},{10,... | collective-permute-start | bytes 589832 | tf_op jit(solution)/shard_map/ppermute | solution.py:332
  230.5 42.5 %all-to-all-start.4 = ((bf16[16,24,2048]{2,1,0:T(8,128)(2,1)}), bf16[16,24,2048]{2,1,0:T(8,128)(2,1)}, u32[]{:S(2)}, u32[]{:S(2)}) async-start(bf16[16,24,2048]{2,1,0:T(8,128)(2,1)} %shard_map.64), calls=%async_computation.4 | async-start | bytes 3145728 | tf_op jit(solution)/shard_map/all_to_all | solution.py:349
  241.3 13.5 %collective-permute-start.30 = (bf16[2,16,2048]{2,1,0:T(8,128)(2,1)}, bf16[2,16,2048]{2,1,0:T(8,128)(2,1)S(1)}, u32[]{:S(2)}, u32[]{:S(2)}) collective-permute-start(bf16[2,16,2048]{2,1,0:T(8,128)(2,1)} %get-tuple-element.90), channel_id=1, source_target_pairs={{0,8},{1,9},{2,10},{3,11},{4,12},{5,13},{6,14},{7,15},{8,0},{9,1},... | collective-permute-start | bytes 393224 | tf_op jit(solution)/shard_map/ppermute | solution.py:332
  245.6 16.8 %collective-permute-start.31 = (bf16[2,16,2048]{2,1,0:T(8,128)(2,1)}, bf16[2,16,2048]{2,1,0:T(8,128)(2,1)S(1)}, u32[]{:S(2)}, u32[]{:S(2)}) collective-permute-start(bf16[2,16,2048]{2,1,0:T(8,128)(2,1)} %get-tuple-element.91), channel_id=1, source_target_pairs={{0,6},{1,7},{2,8},{3,9},{4,10},{5,11},{6,12},{7,13},{8,14},{9,15},... | collective-permute-start | bytes 393224 | tf_op jit(solution)/shard_map/ppermute | solution.py:332
  248.5 18.2 %collective-permute-start.32 = (bf16[2,16,2048]{2,1,0:T(8,128)(2,1)}, bf16[2,16,2048]{2,1,0:T(8,128)(2,1)S(1)}, u32[]{:S(2)}, u32[]{:S(2)}) collective-permute-start(bf16[2,16,2048]{2,1,0:T(8,128)(2,1)} %get-tuple-element.92), channel_id=1, source_target_pairs={{0,10},{1,11},{2,12},{3,13},{4,14},{5,15},{6,0},{7,1},{8,2},{9,3},... | collective-permute-start | bytes 393224 | tf_op jit(solution)/shard_map/ppermute | solution.py:332
  250.7 17.6 %collective-permute-start.33 = (bf16[2,16,2048]{2,1,0:T(8,128)(2,1)}, bf16[2,16,2048]{2,1,0:T(8,128)(2,1)S(1)}, u32[]{:S(2)}, u32[]{:S(2)}) collective-permute-start(bf16[2,16,2048]{2,1,0:T(8,128)(2,1)} %get-tuple-element.93), channel_id=1, source_target_pairs={{0,4},{1,5},{2,6},{3,7},{4,8},{5,9},{6,10},{7,11},{8,12},{9,13},{1... | collective-permute-start | bytes 393224 | tf_op jit(solution)/shard_map/ppermute | solution.py:332
  250.7 17.6 %collective-permute-start.34 = (bf16[2,16,2048]{2,1,0:T(8,128)(2,1)}, bf16[2,16,2048]{2,1,0:T(8,128)(2,1)S(1)}, u32[]{:S(2)}, u32[]{:S(2)}) collective-permute-start(bf16[2,16,2048]{2,1,0:T(8,128)(2,1)} %get-tuple-element.94), channel_id=1, source_target_pairs={{0,12},{1,13},{2,14},{3,15},{4,0},{5,1},{6,2},{7,3},{8,4},{9,5},{1... | collective-permute-start | bytes 393224 | tf_op jit(solution)/shard_map/ppermute | solution.py:332
  254.8 15.4 %collective-permute-start.35 = (bf16[2,16,2048]{2,1,0:T(8,128)(2,1)}, bf16[2,16,2048]{2,1,0:T(8,128)(2,1)S(1)}, u32[]{:S(2)}, u32[]{:S(2)}) collective-permute-start(bf16[2,16,2048]{2,1,0:T(8,128)(2,1)} %get-tuple-element.95), channel_id=1, source_target_pairs={{0,2},{1,3},{2,4},{3,5},{4,6},{5,7},{6,8},{7,9},{8,10},{9,11},{10,... | collective-permute-start | bytes 393224 | tf_op jit(solution)/shard_map/ppermute | solution.py:332
  262.4 7.8 %collective-permute-start.36 = (bf16[2,16,2048]{2,1,0:T(8,128)(2,1)}, bf16[2,16,2048]{2,1,0:T(8,128)(2,1)S(1)}, u32[]{:S(2)}, u32[]{:S(2)}) collective-permute-start(bf16[2,16,2048]{2,1,0:T(8,128)(2,1)} %get-tuple-element.96), channel_id=1, source_target_pairs={{0,14},{1,15},{2,0},{3,1},{4,2},{5,3},{6,4},{7,5},{8,6},{9,7},{10,... | collective-permute-start | bytes 393224 | tf_op jit(solution)/shard_map/ppermute | solution.py:332
  273.0 24.0 %all-to-all-start.5 = ((bf16[16,16,2048]{2,1,0:T(8,128)(2,1)}), bf16[16,16,2048]{2,1,0:T(8,128)(2,1)S(1)}, u32[]{:S(2)}, u32[]{:S(2)}) async-start(bf16[16,16,2048]{2,1,0:T(8,128)(2,1)} %shard_map.67), calls=%async_computation.5 | async-start | bytes 2097152 | tf_op jit(solution)/shard_map/all_to_all | solution.py:349
  (27 other events, 282.8 us)
